TPU v7x, 32 devices: a whole 2x2x4 slice. The times are simulated.
32 devices in a mesh: clip: 16 (over z, x, core), tm: 2 (over y).
Axes of the slice: x: 2, y: 2, z: 4, core: 2. Of those that a mesh axis runs over, the one named last changes fastest.
Arguments:
- block_input: bfloat16 [16, 4, 32, 4096], P('clip', 'tm'), may hold values from -6 to 6
- input_cache: bfloat16 [16, 2, 32, 4096], P('clip'), may hold values from -6 to 6
- middle_cache: bfloat16 [16, 2, 32, 4096], P('clip'), may hold values from -6 to 6
- first_weight: bfloat16 [3, 3, 3, 64, 64], replicated, may hold values from -0.15625 to 0.15625
- first_bias: float32 [64], replicated, may hold values from -3 to 3
- second_weight: bfloat16 [3, 3, 3, 64, 64], replicated, may hold values from -0.15625 to 0.15625
- cotangent: bfloat16 [16, 4, 32, 4096], P('clip', 'tm'), may hold values from -6 to 6
Outputs:
- input_grad: bfloat16 [16, 4, 32, 4096], P('clip', 'tm')
- input_cache_grad: bfloat16 [16, 2, 32, 4096], P('clip', None, 'tm')
- middle_cache_grad: bfloat16 [16, 2, 32, 4096], P('clip', None, 'tm')
- first_weight_grad: float32 [3, 3, 3, 64, 64], replicated
- second_weight_grad: float32 [3, 3, 3, 64, 64], replicated
All inputs are finite; a program needn't handle non-finite values.
Results may differ from a plain program's by a relative error of at most 0.009.
Values may be sent and summed in bfloat16 or wider, within the bound.
No kernel may reach another device: no remote copies, remote signals or barrier semaphores. Data moves between devices by JAX's collectives and lax.ppermute only.
A program may use at most 128 MiB of HBM per device.

v0:
```python
import math

import jax
import jax.numpy as jnp
from jax import lax
from jax.sharding import PartitionSpec as P


def with_halo(cells, sides, width):
    for axis, dim in sides:
        count = lax.axis_size(axis)
        ends = count - 1
        head = lax.slice_in_dim(cells, 0, width, axis=dim)
        tail = lax.slice_in_dim(cells, cells.shape[dim] - width, cells.shape[dim], axis=dim)
        cells = jnp.concatenate(
            [
                lax.ppermute(tail, axis, [(i, (i + 1) % count) for i in range(ends)]),
                cells,
                lax.ppermute(head, axis, [((i + 1) % count, i) for i in range(ends)]),
            ],
            axis=dim,
        )
    return cells


def to_cells(array, chans):
    return array.reshape(
        array.shape[0], array.shape[1], array.shape[2], array.shape[3] // chans, chans
    )


def to_rows(array):
    return array.reshape(
        array.shape[0], array.shape[1], array.shape[2], array.shape[3] * array.shape[4]
    )


def conv_forward(source, weight, row_pad):
    chans = weight.shape[3]
    result = lax.conv_general_dilated(
        to_cells(source, chans),
        weight,
        (1, 1, 1),
        ((0, 0), (row_pad, row_pad), (1, 1)),
        dimension_numbers=("NDHWC", "DHWIO", "NDHWC"),
        preferred_element_type=jnp.float32,
    )
    return to_rows(result)


def conv_input_grad(upstream, weight, row_pad):
    chans = weight.shape[3]
    flipped = jnp.transpose(jnp.flip(weight, (0, 1, 2)), (0, 1, 2, 4, 3))
    result = lax.conv_general_dilated(
        to_cells(upstream, chans),
        flipped,
        (1, 1, 1),
        ((2, 2), (row_pad, row_pad), (1, 1)),
        dimension_numbers=("NDHWC", "DHWIO", "NDHWC"),
        preferred_element_type=jnp.float32,
    )
    return to_rows(result)


def conv_weight_grad(source, upstream, chans, row_pad):
    return lax.conv_general_dilated(
        to_cells(source, chans),
        to_cells(upstream, chans),
        (1, 1, 1),
        ((0, 0), (row_pad, row_pad), (1, 1)),
        dimension_numbers=("CDHWN", "IDHWO", "DHWNC"),
        preferred_element_type=jnp.float32,
    )


def silu_slope(value):
    logistic = jax.nn.sigmoid(value)
    return logistic * (1.0 + value * (1.0 - logistic))


def with_rims(array):
    return with_halo(array, (("tm", 2),), 1)


def body(
    block_input, input_cache, middle_cache, first_weight, first_bias, second_weight, cotangent
):
    chans = first_weight.shape[3]
    width = block_input.shape[3] // chans
    bias_row = jnp.tile(first_bias, width)
    position = lax.axis_index("tm")
    count = (
        block_input.shape[0]
        * lax.axis_size("clip")
        * block_input.shape[1]
        * lax.axis_size("tm")
        * block_input.shape[2]
        * width
    )
    factor = 1.0 / math.sqrt(count)
    band = block_input.shape[2] // lax.axis_size("tm")
    offset = position * band
    second_total = None
    banded_input, banded_upstream = (
        lax.all_to_all(block_input, "tm", split_axis=2, concat_axis=1, tiled=True),
        lax.all_to_all(cotangent, "tm", split_axis=2, concat_axis=1, tiled=True),
    )
    cache_in = lax.dynamic_slice_in_dim(input_cache, offset, band, 2)
    cache_mid = lax.dynamic_slice_in_dim(middle_cache, offset, band, 2)
    extended = jnp.concatenate([cache_in, banded_input], axis=1)
    activated = jax.nn.silu(extended.astype(jnp.float32)).astype(jnp.bfloat16)
    activated_rim = with_rims(activated)
    pre = conv_forward(activated_rim, first_weight, 0) + bias_row
    middle = jax.nn.silu(pre).astype(jnp.bfloat16)
    middle_ext = jnp.concatenate([cache_mid, middle], axis=1)
    middle_ext_grad = conv_input_grad(with_rims(banded_upstream), second_weight, 0)
    second_sum = conv_weight_grad(with_rims(middle_ext), banded_upstream, chans, 0) * factor
    pre_grad = (middle_ext_grad[:, 2:] * silu_slope(pre)).astype(jnp.bfloat16)
    activated_grad = conv_input_grad(with_rims(pre_grad), first_weight, 0)
    first_sum = conv_weight_grad(activated_rim, pre_grad, chans, 0) * factor
    extended_grad = activated_grad * silu_slope(extended.astype(jnp.float32))
    own_grad = (banded_upstream.astype(jnp.float32) + extended_grad[:, 2:]).astype(jnp.bfloat16)
    input_grad = lax.all_to_all(own_grad, "tm", split_axis=1, concat_axis=2, tiled=True)
    input_cache_grad = extended_grad[:, :2].astype(jnp.bfloat16)
    middle_cache_grad = middle_ext_grad[:, :2].astype(jnp.bfloat16)
    first_total, second_total = lax.psum((first_sum, second_sum), ("clip", "tm"))
    return (input_grad, input_cache_grad, middle_cache_grad, first_total, second_total)


def solution(mesh):
    return jax.shard_map(
        body,
        mesh=mesh,
        in_specs=(
            P("clip", "tm", None, None),
            P("clip", None, None, None),
            P("clip", None, None, None),
            P(),
            P(),
            P(),
            P("clip", "tm", None, None),
        ),
        out_specs=(
            P("clip", "tm", None, None),
            P("clip", None, "tm", None),
            P("clip", None, "tm", None),
            P(),
            P(),
        ),
        check_vma=False,
    )
```

profile of v0, /device:TPU:0, one launch (start us, length us, event | category | flops | bytes accessed | tf_op | source)
XLA Modules:
  0.0 343.3 jit_solution(5012771651697742113)
XLA Ops:
  7.2 2.5 copy.135
  9.7 4.4 %all-to-all-start.1 = ((bf16[1,2,32,4096]{3,1,0,2:T(2,128)(2,1)}), bf16[1,2,32,4096]{3,1,0,2:T(2,128)(2,1)S(1)}, u32[]{:S(2)}, u32[]{:S(2)}) async-start(bf16[1,2,32,4096]{3,1,0,2:T(2,128)(2,1)} %copy.135), calls=%async_computation.1 | async-start | bytes 1048576 | tf_op jit(solution)/shard_map/all_to_all | solution.py:105
  17.0 5.9 %all-to-all-done.1 = bf16[1,2,32,4096]{3,1,0,2:T(2,128)(2,1)S(1)} async-done(((bf16[1,2,32,4096]{3,1,0,2:T(2,128)(2,1)}), bf16[1,2,32,4096]{3,1,0,2:T(2,128)(2,1)S(1)}, u32[]{:S(2)}, u32[]{:S(2)}) %all-to-all-start.1) | async-done | bytes 524320 | tf_op jit(solution)/shard_map/all_to_all | solution.py:105
  22.9 3.5 %all-to-all-start = ((bf16[1,2,32,4096]{3,1,0,2:T(2,128)(2,1)}), bf16[1,2,32,4096]{3,1,0,2:T(2,128)(2,1)S(1)}, u32[]{:S(2)}, u32[]{:S(2)}) async-start(bf16[1,2,32,4096]{3,1,0,2:T(2,128)(2,1)} %copy.126), calls=%async_computation | async-start | bytes 1048576 | tf_op jit(solution)/shard_map/all_to_all | solution.py:106
  28.0 3.9 %collective-permute-start.2 = (bf16[1,6,1,4096]{3,2,1,0:T(2,128)(2,1)}, bf16[1,6,1,4096]{3,2,1,0:T(2,128)(2,1)S(1)}, u32[]{:S(2)}, u32[]{:S(2)}) collective-permute-start(bf16[1,6,1,4096]{3,2,1,0:T(2,128)(2,1)} %get-tuple-element.13), channel_id=1, source_target_pairs={{0,1},{2,3},{4,5},{6,7},{8,9},{10,11},{12,13},{14,15},{16,17},{18,... | collective-permute-start | bytes 147464 | tf_op jit(solution)/shard_map/ppermute | solution.py:17
  35.7 4.5 %collective-permute-start = (bf16[1,4,1,4096]{3,2,1,0:T(2,128)(2,1)S(1)}, bf16[1,4,1,4096]{3,2,1,0:T(2,128)(2,1)S(1)}, u32[]{:S(2)}, u32[]{:S(2)}) collective-permute-start(bf16[1,4,1,4096]{3,2,1,0:T(2,128)(2,1)S(1)} %get-tuple-element.19), channel_id=1, source_target_pairs={{0,1},{2,3},{4,5},{6,7},{8,9},{10,11},{12,13},{14,15},{16,17},{18,... | collective-permute-start | bytes 98312 | tf_op jit(solution)/shard_map/ppermute | solution.py:17
  43.7 2.1 concatenate.58
  50.9 13.7 %convolution_select_fusion.1 = f32[6,16,8,9,64]{4,2,3,1,0:T(8,128)S(1)} fusion(bf16[3,3,3,64,64]{4,3,2,1,0:T(8,128)(2,1)S(1)} %copy-done.21, pred[8,9]{0,1:T(8,128)(4,1)S(1)} %copy-done.22, bf16[4,18,1,7,2,64]{5,3,4,1,0,2:T(8,128)(2,1)S(1)} %slice.58, bf16[4,18,1,8,9,64]{5,3,4,1,0,2:T(8,128)(2,1)S(1)} %copy.132), kind=kOutput, calls=%fused_computation.25 | convolution fusion | flops 1022091264 | bytes 2783304 | tf_op jit(solution)/shard_map/conv_general_dilated | solution.py:54
  65.7 2.6 copy.134
  68.3 3.8 %reshape.260 = f32[1,6,16,4096]{3,2,1,0:T(8,128)} reshape(f32[6,16,1,64,64]{4,3,1,0,2:T(8,128)} %copy.134) | data formatting | bytes 3145728 | tf_op jit(solution)/shard_map/reshape | solution.py:33
  76.7 4.7 %fusion.37 = f32[4,16,8,9,64]{4,2,3,1,0:T(8,128)S(1)} fusion(bf16[3,3,3,64,64]{4,3,2,1,0:T(8,128)(2,1)S(1)} %copy-done, bf16[6,18,1,7,2,64]{5,3,4,1,0,2:T(8,128)(2,1)S(1)} %slice.63, bf16[6,18,1,8,9,64]{5,3,4,1,0,2:T(8,128)(2,1)S(1)} %copy.141, pred[8,9]{0,1:T(8,128)(4,1)S(1)} %copy-done.22), kind=kOutput, calls=%fused_computation.44 | convolution fusion | flops 1023160320 | bytes 2589768 | tf_op jit(solution)/shard_map/conv_general_dilated | solution.py:40
  86.3 3.8 %reshape.306 = bf16[1,4,16,64,64]{4,0,3,2,1:T(2,128)(2,1)} reshape(bf16[1,4,16,4096]{3,2,1,0:T(8,128)(2,1)S(1)} %get-tuple-element.10) | data formatting | bytes 1048576 | tf_op jit(solution)/shard_map/reshape | solution.py:27
  91.8 4.9 %collective-permute-start.6 = (bf16[1,6,1,4096]{3,2,1,0:T(2,128)(2,1)}, bf16[1,6,1,4096]{3,2,1,0:T(2,128)(2,1)}, u32[]{:S(2)}, u32[]{:S(2)}) collective-permute-start(bf16[1,6,1,4096]{3,2,1,0:T(2,128)(2,1)} %get-tuple-element.11), channel_id=1, source_target_pairs={{0,1},{2,3},{4,5},{6,7},{8,9},{10,11},{12,13},{14,15},{16,17},{18,... | collective-permute-start | bytes 147464 | tf_op jit(solution)/shard_map/ppermute | solution.py:17
  97.9 5.8 %collective-permute-start.4 = (bf16[1,4,1,4096]{3,2,1,0:T(2,128)(2,1)}, bf16[1,4,1,4096]{3,2,1,0:T(2,128)(2,1)}, u32[]{:S(2)}, u32[]{:S(2)}) collective-permute-start(bf16[1,4,1,4096]{3,2,1,0:T(2,128)(2,1)} %get-tuple-element.15), channel_id=1, source_target_pairs={{0,1},{2,3},{4,5},{6,7},{8,9},{10,11},{12,13},{14,15},{16,17},{18,... | collective-permute-start | bytes 98312 | tf_op jit(solution)/shard_map/ppermute | solution.py:17
  105.2 29.1 %fusion.40 = f32[3,3,3,64,64]{4,3,2,1,0:T(8,128)} fusion(bf16[1,4,16,64,64]{4,0,3,2,1:T(2,128)(2,1)} %reshape.306, bf16[1,6,18,64,64]{4,3,2,1,0:T(8,128)(2,1)} %get-tuple-element.7), kind=kOutput, calls=%fused_computation.45 | convolution fusion | flops 896643072 | bytes 1851392 | tf_op jit(solution)/shard_map/conv_general_dilated | solution.py:66
  139.5 13.7 %convolution_select_fusion = f32[6,16,8,9,64]{4,2,3,1,0:T(8,128)S(1)} fusion(bf16[3,3,3,64,64]{4,3,2,1,0:T(8,128)(2,1)S(1)} %copy-done, pred[8,9]{0,1:T(8,128)(4,1)S(1)} %copy-done.23, bf16[4,18,1,7,2,64]{5,3,4,1,0,2:T(8,128)(2,1)S(1)} %slice.67, bf16[4,18,1,8,9,64]{5,3,4,1,0,2:T(8,128)(2,1)S(1)} %copy.147), kind=kOutput, calls=%fused_computation.24 | convolution fusion | flops 1022091264 | bytes 2783304 | tf_op jit(solution)/shard_map/conv_general_dilated | solution.py:54
  154.2 2.6 copy.149
  156.8 2.5 reshape.263
  162.5 4.0 %reshape.307 = bf16[1,6,18,64,64]{4,0,3,2,1:T(2,128)(2,1)} reshape(bf16[1,6,18,4096]{3,2,1,0:T(8,128)(2,1)S(1)} %pad_maximum_fusion.1) | data formatting | bytes 1769472 | tf_op jit(solution)/shard_map/reshape | solution.py:27
  166.6 30.0 %fusion.43 = f32[3,3,3,64,64]{4,3,2,1,0:T(8,128)} fusion(bf16[1,6,18,64,64]{4,0,3,2,1:T(2,128)(2,1)} %reshape.307, bf16[1,4,16,64,64]{4,3,2,1,0:T(8,128)(2,1)S(1)} %copy-done.11), kind=kOutput, calls=%fused_computation.46 | convolution fusion | flops 896643072 | bytes 1851392 | tf_op jit(solution)/shard_map/conv_general_dilated | solution.py:66
  199.7 4.5 %all-to-all-start.2 = ((bf16[1,4,16,4096]{3,2,0,1:T(8,128)(2,1)}), bf16[1,4,16,4096]{3,2,0,1:T(8,128)(2,1)S(1)}, u32[]{:S(2)}, u32[]{:S(2)}) async-start(bf16[1,4,16,4096]{3,2,0,1:T(8,128)(2,1)} %fusion.51), calls=%async_computation.2 | async-start | bytes 1048576 | tf_op jit(solution)/shard_map/all_to_all | solution.py:123
  207.7 4.3 %all-to-all-done.2 = bf16[1,4,16,4096]{3,2,0,1:T(8,128)(2,1)S(1)} async-done(((bf16[1,4,16,4096]{3,2,0,1:T(8,128)(2,1)}), bf16[1,4,16,4096]{3,2,0,1:T(8,128)(2,1)S(1)}, u32[]{:S(2)}, u32[]{:S(2)}) %all-to-all-start.2) | async-done | bytes 524320 | tf_op jit(solution)/shard_map/all_to_all | solution.py:123
  212.8 120.0 %all-reduce.3.cloned.1.call-done = (f32[3,3,3,64,64]{4,3,2,1,0:T(8,128)}, f32[3,3,3,64,64]{4,3,2,1,0:T(8,128)}) async-done(((f32[3,3,3,64,64]{4,3,2,1,0:T(8,128)}, f32[3,3,3,64,64]{4,3,2,1,0:T(8,128)}), (f32[3,3,3,64,64]{4,3,2,1,0:T(8,128)}, f32[3,3,3,64,64]{4,3,2,1,0:T(8,128)})) %all-reduce.3.cloned.1.call-update) | async-done | bytes 884752 | tf_op jit(solution)/shard_map/psum | solution.py:126
  332.8 2.3 copy.177
  (117 shorter events, 49.2 us)
Async XLA Ops:
  7.2 69.5 %copy-start = (bf16[3,3,3,64,64]{4,3,2,1,0:T(8,128)(2,1)S(1)}, bf16[3,3,3,64,64]{4,3,2,1,0:T(8,128)(2,1)}, u32[]{:S(2)}) copy-start(bf16[3,3,3,64,64]{4,3,2,1,0:T(8,128)(2,1)} %param.10) | copy-start | bytes 663556
  7.2 6.9 %copy-start.19 = (bf16[1,2,32,4096]{3,2,1,0:T(8,128)(2,1)S(1)}, bf16[1,2,32,4096]{3,2,1,0:T(8,128)(2,1)}, u32[]{:S(2)}) copy-start(bf16[1,2,32,4096]{3,2,1,0:T(8,128)(2,1)} %param.8) | copy-start | bytes 1572868
  7.2 6.9 %copy-start.18 = (bf16[1,2,32,4096]{3,2,1,0:T(8,128)(2,1)S(1)}, bf16[1,2,32,4096]{3,2,1,0:T(8,128)(2,1)}, u32[]{:S(2)}) copy-start(bf16[1,2,32,4096]{3,2,1,0:T(8,128)(2,1)} %param.9) | copy-start | bytes 1572868
  7.2 8.3 %copy-start.17 = (bf16[1,2,32,4096]{3,2,1,0:T(8,128)(2,1)S(1)}, bf16[1,2,32,4096]{3,2,1,0:T(8,128)(2,1)}, u32[]{:S(2)}) copy-start(bf16[1,2,32,4096]{3,2,1,0:T(8,128)(2,1)} %param.13) | copy-start | bytes 1572868
  9.7 7.1 %copy-start.20 = (f32[64]{0:T(128)S(1)}, f32[64]{0:T(128)}, u32[]{:S(2)}) copy-start(f32[64]{0:T(128)} %param.11) | copy-start | bytes 772
  9.7 13.1 %all-to-all-start.1 = ((bf16[1,2,32,4096]{3,1,0,2:T(2,128)(2,1)}), bf16[1,2,32,4096]{3,1,0,2:T(2,128)(2,1)S(1)}, u32[]{:S(2)}, u32[]{:S(2)}) async-start(bf16[1,2,32,4096]{3,1,0,2:T(2,128)(2,1)} %copy.135), calls=%async_computation.1 | async-start | bytes 1048576 | tf_op jit(solution)/shard_map/all_to_all | solution.py:105
  14.2 12.5 %copy-start.12 = (bf16[1,2,16,4096]{3,2,1,0:T(8,128)(2,1)}, bf16[1,2,16,4096]{3,2,1,0:T(8,128)(2,1)S(1)}, u32[]{:S(2)}) copy-start(bf16[1,2,16,4096]{3,2,1,0:T(8,128)(2,1)S(1)} %get-tuple-element.24) | copy-start | bytes 786436
  14.2 76.7 %copy-start.14 = (bf16[1,2,16,4096]{3,2,1,0:T(8,128)(2,1)}, bf16[1,2,16,4096]{3,2,1,0:T(8,128)(2,1)S(1)}, u32[]{:S(2)}) copy-start(bf16[1,2,16,4096]{3,2,1,0:T(8,128)(2,1)S(1)} %get-tuple-element.23) | copy-start | bytes 786436
  22.9 12.4 %all-to-all-start = ((bf16[1,2,32,4096]{3,1,0,2:T(2,128)(2,1)}), bf16[1,2,32,4096]{3,1,0,2:T(2,128)(2,1)S(1)}, u32[]{:S(2)}, u32[]{:S(2)}) async-start(bf16[1,2,32,4096]{3,1,0,2:T(2,128)(2,1)} %copy.126), calls=%async_computation | async-start | bytes 1048576 | tf_op jit(solution)/shard_map/all_to_all | solution.py:106
  26.4 306.5 %all-reduce.3.cloned.1.call-start = ((), (), s32[]{:S(2)}) async-start(), calls=%async_computation.3 | async-start | bytes 3538944 | tf_op jit(solution)/shard_map/psum | solution.py:126
  26.7 8.6 %copy-start.2 = (bf16[1,2,2,16,4096]{4,3,1,2,0:T(8,128)(2,1)}, bf16[1,2,2,16,4096]{4,3,1,2,0:T(8,128)(2,1)S(1)}, u32[]{:S(2)}) copy-start(bf16[1,2,2,16,4096]{4,3,1,2,0:T(8,128)(2,1)S(1)} %copy.173) | copy-start | bytes 1572868
  28.0 44.1 %collective-permute-start.2 = (bf16[1,6,1,4096]{3,2,1,0:T(2,128)(2,1)}, bf16[1,6,1,4096]{3,2,1,0:T(2,128)(2,1)S(1)}, u32[]{:S(2)}, u32[]{:S(2)}) collective-permute-start(bf16[1,6,1,4096]{3,2,1,0:T(2,128)(2,1)} %get-tuple-element.13), channel_id=1, source_target_pairs={{0,1},{2,3},{4,5},{6,7},{8,9},{10,11},{12,13},{14,15},{16,17},{18,... | collective-permute-start | bytes 147464 | tf_op jit(solution)/shard_map/ppermute | solution.py:17
  31.9 40.6 %collective-permute-start.3 = (bf16[1,6,1,4096]{3,2,1,0:T(2,128)(2,1)}, bf16[1,6,1,4096]{3,2,1,0:T(2,128)(2,1)S(1)}, u32[]{:S(2)}, u32[]{:S(2)}) collective-permute-start(bf16[1,6,1,4096]{3,2,1,0:T(2,128)(2,1)} %get-tuple-element.14), channel_id=1, source_target_pairs={{1,0},{3,2},{5,4},{7,6},{9,8},{11,10},{13,12},{15,14},{17,16},{19,... | collective-permute-start | bytes 147464 | tf_op jit(solution)/shard_map/ppermute | solution.py:19
  35.3 6.5 %copy-start.10 = (bf16[1,4,16,64,64]{4,3,2,1,0:T(8,128)(2,1)S(1)}, bf16[1,4,16,64,64]{4,3,2,1,0:T(8,128)(2,1)}, u32[]{:S(2)}) copy-start(bf16[1,4,16,64,64]{4,3,2,1,0:T(8,128)(2,1)} %concatenate.65) | copy-start | bytes 1572868
  35.6 10.2 %copy-start.4 = (bf16[1,2,2,16,4096]{4,3,1,2,0:T(8,128)(2,1)}, bf16[1,2,2,16,4096]{4,3,1,2,0:T(8,128)(2,1)S(1)}, u32[]{:S(2)}) copy-start(bf16[1,2,2,16,4096]{4,3,1,2,0:T(8,128)(2,1)S(1)} %copy.174) | copy-start | bytes 1572868
  35.7 10.1 %collective-permute-start = (bf16[1,4,1,4096]{3,2,1,0:T(2,128)(2,1)S(1)}, bf16[1,4,1,4096]{3,2,1,0:T(2,128)(2,1)S(1)}, u32[]{:S(2)}, u32[]{:S(2)}) collective-permute-start(bf16[1,4,1,4096]{3,2,1,0:T(2,128)(2,1)S(1)} %get-tuple-element.19), channel_id=1, source_target_pairs={{0,1},{2,3},{4,5},{6,7},{8,9},{10,11},{12,13},{14,15},{16,17},{18,... | collective-permute-start | bytes 98312 | tf_op jit(solution)/shard_map/ppermute | solution.py:17
  40.3 6.2 %collective-permute-start.1 = (bf16[1,4,1,4096]{3,2,1,0:T(2,128)(2,1)S(1)}, bf16[1,4,1,4096]{3,2,1,0:T(2,128)(2,1)S(1)}, u32[]{:S(2)}, u32[]{:S(2)}) collective-permute-start(bf16[1,4,1,4096]{3,2,1,0:T(2,128)(2,1)S(1)} %get-tuple-element.20), channel_id=1, source_target_pairs={{1,0},{3,2},{5,4},{7,6},{9,8},{11,10},{13,12},{15,14},{17,16},{19,... | collective-permute-start | bytes 98312 | tf_op jit(solution)/shard_map/ppermute | solution.py:19
  86.3 5.5 %copy-start.6 = (bf16[1,4,16,4096]{3,2,1,0:T(8,128)(2,1)}, bf16[1,4,16,4096]{3,2,1,0:T(8,128)(2,1)S(1)}, u32[]{:S(2)}) copy-start(bf16[1,4,16,4096]{3,2,1,0:T(8,128)(2,1)S(1)} %get-tuple-element.10) | copy-start | bytes 1572868
  91.8 69.3 %collective-permute-start.6 = (bf16[1,6,1,4096]{3,2,1,0:T(2,128)(2,1)}, bf16[1,6,1,4096]{3,2,1,0:T(2,128)(2,1)}, u32[]{:S(2)}, u32[]{:S(2)}) collective-permute-start(bf16[1,6,1,4096]{3,2,1,0:T(2,128)(2,1)} %get-tuple-element.11), channel_id=1, source_target_pairs={{0,1},{2,3},{4,5},{6,7},{8,9},{10,11},{12,13},{14,15},{16,17},{18,... | collective-permute-start | bytes 147464 | tf_op jit(solution)/shard_map/ppermute | solution.py:17
  96.6 64.5 %collective-permute-start.7 = (bf16[1,6,1,4096]{3,2,1,0:T(2,128)(2,1)}, bf16[1,6,1,4096]{3,2,1,0:T(2,128)(2,1)}, u32[]{:S(2)}, u32[]{:S(2)}) collective-permute-start(bf16[1,6,1,4096]{3,2,1,0:T(2,128)(2,1)} %get-tuple-element.12), channel_id=1, source_target_pairs={{1,0},{3,2},{5,4},{7,6},{9,8},{11,10},{13,12},{15,14},{17,16},{19,... | collective-permute-start | bytes 147464 | tf_op jit(solution)/shard_map/ppermute | solution.py:19
  97.9 36.4 %collective-permute-start.4 = (bf16[1,4,1,4096]{3,2,1,0:T(2,128)(2,1)}, bf16[1,4,1,4096]{3,2,1,0:T(2,128)(2,1)}, u32[]{:S(2)}, u32[]{:S(2)}) collective-permute-start(bf16[1,4,1,4096]{3,2,1,0:T(2,128)(2,1)} %get-tuple-element.15), channel_id=1, source_target_pairs={{0,1},{2,3},{4,5},{6,7},{8,9},{10,11},{12,13},{14,15},{16,17},{18,... | collective-permute-start | bytes 98312 | tf_op jit(solution)/shard_map/ppermute | solution.py:17
  103.7 30.6 %collective-permute-start.5 = (bf16[1,4,1,4096]{3,2,1,0:T(2,128)(2,1)}, bf16[1,4,1,4096]{3,2,1,0:T(2,128)(2,1)}, u32[]{:S(2)}, u32[]{:S(2)}) collective-permute-start(bf16[1,4,1,4096]{3,2,1,0:T(2,128)(2,1)} %get-tuple-element.16), channel_id=1, source_target_pairs={{1,0},{3,2},{5,4},{7,6},{9,8},{11,10},{13,12},{15,14},{17,16},{19,... | collective-permute-start | bytes 98312 | tf_op jit(solution)/shard_map/ppermute | solution.py:19
  105.1 29.2 %copy-start.7 = (bf16[1,4,16,4096]{3,2,1,0:T(8,128)(2,1)S(1)}, bf16[1,4,16,4096]{3,2,1,0:T(8,128)(2,1)}, u32[]{:S(2)}) copy-start(bf16[1,4,16,4096]{3,2,1,0:T(8,128)(2,1)} %copy-done.6) | copy-start | bytes 1572868
  199.7 12.3 %all-to-all-start.2 = ((bf16[1,4,16,4096]{3,2,0,1:T(8,128)(2,1)}), bf16[1,4,16,4096]{3,2,0,1:T(8,128)(2,1)S(1)}, u32[]{:S(2)}, u32[]{:S(2)}) async-start(bf16[1,4,16,4096]{3,2,0,1:T(8,128)(2,1)} %fusion.51), calls=%async_computation.2 | async-start | bytes 1048576 | tf_op jit(solution)/shard_map/all_to_all | solution.py:123
  (12 other events, 27.3 us)
Sparse Core Ops, SparseCore 0:
  196.7 136.1 all-reduce.2
where the time goes:
time: 348 us; the launch traced here: 343 us
  waiting for transfers between devices  131 us (38%)
  matrix products  91.3 us (26%)
  local copies, waits for them, and re-layouts  53.5 us (15%)
  starting transfers between devices  37 us (11%)
  other arithmetic  16 us (5%)
  between operations  15 us (4%)
    psum x1, waiting for transfers between devices, body(): lax.psum((first_sum, second_sum), ('clip', 'tm'))  120 us
    conv_general_dilated x2, matrix products, conv_weight_grad(): lax.conv_general_dilated(to_cells(source, chans), to_cells(upstream, chan...  59.1 us
    conv_general_dilated x2, matrix products, conv_input_grad(): lax.conv_general_dilated(to_cells(upstream, chans), flipped, (1, 1, 1), (...  27.4 us
    ppermute x4, starting transfers between devices, with_halo(): lax.ppermute(tail, axis, [(i, (i + 1) % count) for i in range(ends)])  19 us
    unnamed x55, local copies, waits for them, and re-layouts  12.6 us
    reshape x4, local copies, waits for them, and re-layouts, to_cells(): array.reshape(array.shape[0], array.shape[1], array.shape[2], array.shape...  9.73 us
    reshape x3, local copies, waits for them, and re-layouts, to_rows(): array.reshape(array.shape[0], array.shape[1], array.shape[2], array.shape...  7.91 us
    conv_general_dilated x10, local copies, waits for them, and re-layouts, conv_input_grad(): lax.conv_general_dilated(to_cells(upstream, chans), flipped, (1, 1, 1), (...  7.71 us
  transfers between devices with their start and end apart: 12, of which 4 were waited for; matrix products, arithmetic and copies ran while one was open for 29% of the time, Pallas kernels for 0%

commit v1 on v0

v1 whole, which is shorter than its diff:
```python
import functools
import math

import jax
import jax.numpy as jnp
from jax import lax
from jax.experimental import pallas as pl
from jax.experimental.pallas import tpu as pltpu
from jax.sharding import PartitionSpec as P

F32 = jnp.float32
BF16 = jnp.bfloat16
OUT = 256
WIN = 384
VMEM = pl.BlockSpec(memory_space=pltpu.VMEM)
SMEM = pl.BlockSpec(memory_space=pltpu.SMEM)
PARAMS = pltpu.CompilerParams(vmem_limit_bytes=60 * 1024 * 1024)


def logistic(value):
    return 1.0 / (1.0 + jnp.exp(-value))


def slope_of(value):
    s = logistic(value)
    return s * (1.0 + value * (1.0 - s))


def row_shifts(value):
    rows = value.shape[0]
    row = lax.broadcasted_iota(jnp.int32, value.shape, 0)
    down = jnp.where(row == 0, 0.0, pltpu.roll(value, 1, axis=0))
    up = jnp.where(row == rows - 1, 0.0, pltpu.roll(value, rows - 1, axis=0))
    return down, value, up


def column_shift(value, chans):
    pad = jnp.zeros((value.shape[0], 2 * chans), value.dtype)
    return pltpu.roll(jnp.concatenate([value, pad], axis=1), chans, axis=1)


def put_shifted(ref, frame, value, chans):
    for k, part in enumerate(row_shifts(column_shift(value, chans))):
        ref[frame, k] = part.astype(BF16)


def banded(weight):
    chans = weight.shape[3]
    left = jnp.pad(weight, ((0, 0), (0, 0), (0, 1), (0, 0), (0, 0)))
    right = jnp.pad(weight, ((0, 0), (0, 0), (1, 0), (0, 0), (0, 0)))
    pair = jnp.concatenate([left, right], axis=-1).reshape(9, 4 * chans, 2 * chans)
    low = jnp.pad(pair, ((0, 0), (0, 2 * chans), (0, 0)))
    high = jnp.pad(pair, ((0, 0), (2 * chans, 0), (0, 0)))
    return jnp.concatenate([low, high], axis=-1).reshape(9 * WIN, OUT)


def conv_frame(ref, weight_ref, frame, taps=(0, 1, 2)):
    groups = (ref.shape[3] - 2 * OUT // 4) // OUT
    pieces = []
    for kt in taps:
        for kr in range(3):
            pieces.append(
                jnp.concatenate(
                    [ref[frame + kt, kr, :, OUT * j : OUT * j + WIN] for j in range(groups)],
                    axis=0,
                )
            )
    lhs = jnp.concatenate(pieces, axis=1)
    rhs = weight_ref[taps[0] * 3 * WIN : (taps[-1] + 1) * 3 * WIN, :]
    return jnp.dot(lhs, rhs, preferred_element_type=F32)


def first_kernel(
    chans,
    flag_ref,
    x_ref,
    back_ref,
    cache_ref,
    cot_ref,
    ahead_ref,
    w_first_ref,
    w_second_ref,
    bias_ref,
    pre_grad_ref,
    middle_ref,
    cache_grad_ref,
    act_ref,
    shifted_act,
    shifted_cot,
    slope_ref,
):
    frames, rows = x_ref.shape[0], x_ref.shape[1]
    groups = x_ref.shape[2] // OUT
    first = flag_ref[0] == 0

    def silu(value):
        value = value.astype(F32)
        return (value * logistic(value)).astype(BF16).astype(F32)

    @pl.when(first)
    def _():
        @pl.loop(0, 2)
        def _(f):
            put_shifted(shifted_act, f, silu(cache_ref[f]), chans)

    @pl.when(jnp.logical_not(first))
    def _():
        @pl.loop(0, 2)
        def _(f):
            put_shifted(shifted_act, f, silu(back_ref[f]), chans)

    @pl.loop(0, frames)
    def _(f):
        put_shifted(shifted_act, f + 2, silu(x_ref[f]), chans)
        put_shifted(shifted_cot, f, cot_ref[f].astype(F32), chans)

    @pl.loop(0, 2)
    def _(f):
        put_shifted(shifted_cot, f + frames, ahead_ref[f].astype(F32), chans)

    @pl.loop(0, frames + 2)
    def _(f):
        act_ref[f] = shifted_act[f, 1]

    @pl.loop(0, frames)
    def _(f):
        pre = conv_frame(shifted_act, w_first_ref, f) + bias_ref[...]
        s = logistic(pre)
        slope_ref[...] = s * (1.0 + pre * (1.0 - s))
        middle = (pre * s).astype(BF16)
        for j in range(groups):
            middle_ref[f, :, OUT * j : OUT * (j + 1)] = middle[rows * j : rows * (j + 1)]
        grad = conv_frame(shifted_cot, w_second_ref, f)
        pre_grad = (grad * slope_ref[...]).astype(BF16)
        for j in range(groups):
            pre_grad_ref[f, :, OUT * j : OUT * (j + 1)] = pre_grad[rows * j : rows * (j + 1)]

    for f in range(2):
        grad = conv_frame(shifted_cot, w_second_ref, f - 2, taps=(1, 2) if f else (2,))
        grad = grad.astype(BF16)
        for j in range(groups):
            cache_grad_ref[f, :, OUT * j : OUT * (j + 1)] = grad[rows * j : rows * (j + 1)]


def sums_kernel(
    chans,
    flag_ref,
    act_ref,
    pre_grad_ref,
    middle_ref,
    middle_cache_ref,
    cot_ref,
    ahead_ref,
    out_ref,
    mid,
    shifted_cot,
    shifted_grad,
    total_first,
    total_second,
):
    frames, rows = middle_ref.shape[0], middle_ref.shape[1]
    groups = middle_ref.shape[2] // OUT
    first = flag_ref[0] == 0

    @pl.loop(0, 2)
    def _(f):
        value = jnp.where(first, middle_cache_ref[f].astype(F32), 0.0)
        mid[f] = column_shift(value, chans).astype(BF16)

    @pl.loop(0, frames)
    def _(f):
        mid[f + 2] = column_shift(middle_ref[f].astype(F32), chans).astype(BF16)
        for k, part in enumerate(row_shifts(cot_ref[f].astype(F32))):
            shifted_cot[f, 2 - k] = part.astype(BF16)
        for k, part in enumerate(row_shifts(pre_grad_ref[f].astype(F32))):
            shifted_grad[f, 2 - k] = part.astype(BF16)

    @pl.loop(0, 2)
    def _(f):
        for k, part in enumerate(row_shifts(ahead_ref[f].astype(F32))):
            shifted_cot[f + frames, 2 - k] = part.astype(BF16)

    def correlate(source, upstream, pairs):
        left = jnp.concatenate(
            [source[a, :, OUT * j : OUT * j + WIN] for a, _ in pairs for j in range(groups)],
            axis=0,
        )
        right = jnp.concatenate(
            [
                jnp.concatenate(
                    [upstream[t, k, :, OUT * j : OUT * (j + 1)] for _, t in pairs for j in range(groups)],
                    axis=0,
                )
                for k in range(3)
            ],
            axis=1,
        )
        return lax.dot_general(
            left, right, (((0,), (0,)), ((), ())), preferred_element_type=F32
        )

    lane = lax.broadcasted_iota(jnp.int32, (chans, 2 * chans), 1) < chans

    def tap(total, kr, kq):
        cut = lambda d: total[
            chans * (kq + d) : chans * (kq + d + 1),
            OUT * kr + 2 * chans * (d // 2) : OUT * kr + 2 * chans * (d // 2 + 1),
        ]
        value = jnp.where(lane, cut(0) + cut(2), cut(1) + cut(3))
        return value + pltpu.roll(value, chans, axis=1)

    for kt in range(3):
        total_first[...] = correlate(act_ref, shifted_grad, [(t + kt, t) for t in range(frames)])
        total_second[...] = correlate(
            mid, shifted_cot, [(a, a - kt) for a in range(kt, frames + 2)]
        )
        for kr in range(3):
            for kq in range(3):
                at = ((kt * 3 + kr) * 3 + kq) * chans
                out_ref[at : at + chans, :] = jnp.where(
                    lane, tap(total_first, kr, kq), tap(total_second, kr, kq)
                ).astype(BF16)


def last_kernel(
    chans,
    x_ref,
    cache_ref,
    cot_ref,
    pre_grad_ref,
    ahead_ref,
    w_first_ref,
    input_grad_ref,
    cache_grad_ref,
    shifted,
):
    frames, rows = x_ref.shape[0], x_ref.shape[1]
    groups = x_ref.shape[2] // OUT

    @pl.loop(0, frames)
    def _(f):
        put_shifted(shifted, f, pre_grad_ref[f].astype(F32), chans)

    @pl.loop(0, 2)
    def _(f):
        put_shifted(shifted, f + frames, ahead_ref[f].astype(F32), chans)

    @pl.loop(0, frames)
    def _(f):
        grad = conv_frame(shifted, w_first_ref, f)
        for j in range(groups):
            cut = slice(OUT * j, OUT * (j + 1))
            value = grad[rows * j : rows * (j + 1)] * slope_of(x_ref[f, :, cut].astype(F32))
            input_grad_ref[f, :, cut] = (cot_ref[f, :, cut].astype(F32) + value).astype(BF16)

    for f in range(2):
        grad = conv_frame(shifted, w_first_ref, f - 2, taps=(1, 2) if f else (2,))
        for j in range(groups):
            cut = slice(OUT * j, OUT * (j + 1))
            value = grad[rows * j : rows * (j + 1)] * slope_of(cache_ref[f, :, cut].astype(F32))
            cache_grad_ref[f, :, cut] = value.astype(BF16)


def call(kernel, name, out_shape, scratch, n_smem, flops, args):
    moved = sum(a.size * a.dtype.itemsize for a in args)
    moved += sum(o.size * o.dtype.itemsize for o in jax.tree.leaves(out_shape))
    return pl.pallas_call(
        kernel,
        out_shape=out_shape,
        in_specs=[SMEM] * n_smem + [VMEM] * (len(args) - n_smem),
        out_specs=jax.tree.map(lambda _: VMEM, out_shape),
        scratch_shapes=scratch,
        compiler_params=PARAMS,
        cost_estimate=pl.CostEstimate(flops=flops, bytes_accessed=moved, transcendentals=0),
        name=name,
    )(*args)


def to_row_parts(grad, count):
    rows = grad.shape[1] // count
    mine = grad[:, :rows]
    place = lax.axis_index("tm")
    for k in range(1, count):
        part = lax.ppermute(grad[:, k * rows : (k + 1) * rows], "tm", [(0, k)])
        mine = jnp.where(place == k, part, mine)
    return mine[None]


def body(
    block_input, input_cache, middle_cache, first_weight, first_bias, second_weight, cotangent
):
    chans = first_weight.shape[3]
    tm, clips = lax.axis_size("tm"), lax.axis_size("clip")
    _, frames, rows, lanes = block_input.shape
    width = lanes // chans
    factor = 1.0 / math.sqrt(block_input.shape[0] * clips * frames * tm * rows * width)
    x, cot = block_input[0], cotangent[0]
    icache, mcache = input_cache[0], middle_cache[0]
    place = lax.axis_index("tm").astype(jnp.int32).reshape(1)
    onward = [(i, i + 1) for i in range(tm - 1)]
    backward = [(i + 1, i) for i in range(tm - 1)]
    back = lax.ppermute(x[frames - 2 :], "tm", onward)
    ahead = lax.ppermute(cot[:2], "tm", backward)

    def turned(weight):
        return jnp.transpose(jnp.flip(weight, (0, 1, 2)), (0, 1, 2, 4, 3))

    w_first, w_second = banded(first_weight), banded(turned(second_weight))
    w_first_turned = banded(turned(first_weight))
    bias = jnp.tile(first_bias, OUT // chans).reshape(1, OUT)

    padded = lanes + 2 * chans
    shape = lambda n, l=lanes: jax.ShapeDtypeStruct((n, rows, l), BF16)
    tap_flops = 2 * rows * width * 9 * chans * chans * 3
    pre_grad, middle, mid_cache_grad, act = call(
        functools.partial(first_kernel, chans),
        "first",
        (shape(frames), shape(frames), shape(2), shape(frames + 2, padded)),
        [
            pltpu.VMEM((frames + 2, 3, rows, padded), BF16),
            pltpu.VMEM((frames + 2, 3, rows, padded), BF16),
            pltpu.VMEM((rows * lanes // OUT, OUT), F32),
        ],
        1,
        tap_flops * 15,
        (place, x, back, icache, cot, ahead, w_first, w_second, bias),
    )
    grad_ahead = lax.ppermute(pre_grad[:2], "tm", backward)
    sums = call(
        functools.partial(sums_kernel, chans),
        "sums",
        jax.ShapeDtypeStruct((27 * chans, 2 * chans), BF16),
        [
            pltpu.VMEM((frames + 2, rows, padded), BF16),
            pltpu.VMEM((frames + 2, 3, rows, lanes), BF16),
            pltpu.VMEM((frames, 3, rows, lanes), BF16),
            pltpu.VMEM((WIN, 3 * OUT), F32),
            pltpu.VMEM((WIN, 3 * OUT), F32),
        ],
        1,
        tap_flops * 15,
        (place, act, pre_grad, middle, mcache, cot, ahead),
    )
    everyone = ("clip", "tm")
    count = clips * tm
    height = sums.shape[0]
    share = -(-height // count)
    padded_sums = jnp.pad(sums, ((0, share * count - height), (0, 0)))
    parts = lax.all_to_all(
        padded_sums.reshape(count, share, 2 * chans), everyone, 0, 0, tiled=True
    )
    mine = (jnp.sum(parts.astype(F32), axis=0) * factor).astype(BF16)
    whole = lax.all_to_all(
        jnp.broadcast_to(mine[None], (count, share, 2 * chans)), everyone, 0, 0, tiled=True
    )
    whole = whole.reshape(count * share, 2 * chans)[:height].reshape(3, 3, 3, chans, 2 * chans)
    first_total = whole[..., :chans].astype(F32)
    second_total = whole[..., chans:].astype(F32)

    input_grad, in_cache_grad = call(
        functools.partial(last_kernel, chans),
        "last",
        (shape(frames), shape(2)),
        [pltpu.VMEM((frames + 2, 3, rows, padded), BF16)],
        0,
        tap_flops * 9,
        (x, icache, cot, pre_grad, grad_ahead, w_first_turned),
    )
    return (
        input_grad[None],
        to_row_parts(in_cache_grad, tm),
        to_row_parts(mid_cache_grad, tm),
        first_total,
        second_total,
    )


def solution(mesh):
    return jax.shard_map(
        body,
        mesh=mesh,
        in_specs=(
            P("clip", "tm", None, None),
            P("clip", None, None, None),
            P("clip", None, None, None),
            P(),
            P(),
            P(),
            P("clip", "tm", None, None),
        ),
        out_specs=(
            P("clip", "tm", None, None),
            P("clip", None, "tm", None),
            P("clip", None, "tm", None),
            P(),
            P(),
        ),
        check_vma=False,
    )
```

time: 348 us -> 90 us (0.26); the launches traced: 343 us -> 89 us
  waiting for transfers between devices: 131 us -> 15.8 us
  matrix products: 91.3 us -> 0 us
  local copies, waits for them, and re-layouts: 53.5 us -> 8.74 us
  Pallas kernels: 0 us -> 27.9 us
  between operations: 15 us -> 0.8 us
  starting transfers between devices: 37 us -> 26.3 us
  other arithmetic: 16 us -> 9.42 us
    psum x1 -> x0, waiting for transfers between devices: 120 us -> none  [body(): lax.psum((first_sum, second_sum), ('clip', 'tm'))]
    conv_general_dilated x5 -> x0, matrix products: 91.3 us -> none  [the longest x2 59.1 us: conv_weight_grad(): lax.conv_general_dilated(to_cells(source, chans), to_cells(upstream, chan...]
    pallas_call x0 -> x3, Pallas kernels: none -> 27.9 us  [call(): pl.pallas_call(kernel, out_shape=out_shape, in_specs=[SMEM] * n_smem + [V...]
    reshape x7 -> x1, local copies, waits for them, and re-layouts: 17.6 us -> 1.96 us  [body(): padded_sums.reshape(count, share, 2 * chans)]
    unnamed x55 -> x16, local copies, waits for them, and re-layouts: 12.6 us -> 3.11 us
    conv_general_dilated x15 -> x0, local copies, waits for them, and re-layouts: 9.29 us -> none  [the longest x10 7.71 us: conv_input_grad(): lax.conv_general_dilated(to_cells(upstream, chans), flipped, (1, 1, 1), (...]
    ppermute x8 -> x5, starting transfers between devices: 24.6 us -> 15.8 us  [the longest x2 8.11 us: to_row_parts(): part = lax.ppermute(grad[:, k * rows:(k + 1) * rows], 'tm', [(0, k)])]
    concatenate x9 -> x0, local copies, waits for them, and re-layouts: 7.19 us -> none  [the longest x7 3.76 us: with_halo(): jnp.concatenate([lax.ppermute(tail, axis, [(i, (i + 1) % count) for i in...]
  transfers between devices with their start and end apart: 12 -> 7, of which waited for: 4 -> 4; matrix products, arithmetic and copies ran while one was open for 29% -> 17% of each run, Pallas kernels for 0% -> 19%
where the time goes in v1:
time: 90 us; the launch traced here: 89 us
  Pallas kernels  27.9 us (31%)
  starting transfers between devices  26.3 us (29%)
  waiting for transfers between devices  15.8 us (18%)
  other arithmetic  9.42 us (10%)
  local copies, waits for them, and re-layouts  8.74 us (10%)
    pallas_call x3, Pallas kernels, call(): pl.pallas_call(kernel, out_shape=out_shape, in_specs=[SMEM] * n_smem + [V...  27.9 us
    all_to_all x1, waiting for transfers between devices, body(): lax.all_to_all(jnp.broadcast_to(mine[None], (count, share, 2 * chans)), e...  12.8 us
    ppermute x2, starting transfers between devices, to_row_parts(): part = lax.ppermute(grad[:, k * rows:(k + 1) * rows], 'tm', [(0, k)])  8.11 us
    all_to_all x1, starting transfers between devices, body(): lax.all_to_all(padded_sums.reshape(count, share, 2 * chans), everyone, 0,...  5.89 us
    ppermute x1, starting transfers between devices, body(): back = lax.ppermute(x[frames - 2:], 'tm', onward)  4.97 us
    all_to_all x1, starting transfers between devices, body(): lax.all_to_all(jnp.broadcast_to(mine[None], (count, share, 2 * chans)), e...  4.62 us
    concatenate x3, other arithmetic, banded(): return jnp.concatenate([low, high], axis=-1).reshape(9 * WIN, OUT)  4.31 us
    unnamed x16, local copies, waits for them, and re-layouts  3.11 us
  transfers between devices with their start and end apart: 7, of which 4 were waited for; matrix products, arithmetic and copies ran while one was open for 17% of the time, Pallas kernels for 19%

profile of v1, /device:TPU:0, one launch (start us, length us, event | category | flops | bytes accessed | tf_op | source)
XLA Modules:
  0.0 89.0 jit_solution(275159524173263190)
XLA Ops:
  0.6 1.4 %collective-permute-start.1 = (bf16[2,32,4096]{2,1,0:T(8,128)(2,1)}, bf16[2,32,4096]{2,1,0:T(8,128)(2,1)S(1)}, u32[]{:S(2)}, u32[]{:S(2)}) collective-permute-start(bf16[2,32,4096]{2,1,0:T(8,128)(2,1)} %bitcast.32), channel_id=1, source_target_pairs={{1,0},{3,2},{5,4},{7,6},{9,8},{11,10},{13,12},{15,14},{17,16},{19,... | collective-permute-start | bytes 1572872 | tf_op jit(solution)/shard_map/ppermute | solution.py:303
  2.1 5.0 %collective-permute-start = (bf16[2,32,4096]{2,1,0:T(8,128)(2,1)}, bf16[2,32,4096]{2,1,0:T(8,128)(2,1)S(1)}, u32[]{:S(2)}, u32[]{:S(2)}) collective-permute-start(bf16[2,32,4096]{2,1,0:T(8,128)(2,1)} %bitcast.27), channel_id=1, source_target_pairs={{0,1},{2,3},{4,5},{6,7},{8,9},{10,11},{12,13},{14,15},{16,17},{18,... | collective-permute-start | bytes 1572872 | tf_op jit(solution)/shard_map/ppermute | solution.py:302
  7.1 1.5 %fusion.15 = bf16[3,3,4,64,128]{4,3,2,1,0:T(8,128)(2,1)S(1)} fusion(bf16[3,3,3,64,64]{4,3,2,1,0:T(8,128)(2,1)} %param.10), kind=kLoop, calls=%fused_computation.20 | loop fusion | flops 2359296 | bytes 811008 | tf_op jit(solution)/shard_map/concatenate | solution.py:51
  8.5 1.3 %copy.13 = bf16[3,3,3,64,64]{3,4,2,1,0:T(8,128)(2,1)S(1)} copy(bf16[3,3,3,64,64]{4,3,2,1,0:T(8,128)(2,1)} %param.10) | data formatting | bytes 442368 | tf_op args[3]
  10.4 1.4 %fusion.7 = bf16[9,384,256]{2,1,0:T(8,128)(2,1)} fusion(bf16[9,256,128]{2,1,0:T(8,128)(2,1)S(1)} %bitcast.22), kind=kLoop, calls=%fused_computation.9 | loop fusion | flops 7077888 | bytes 2359296 | tf_op jit(solution)/shard_map/concatenate | solution.py:54
  12.9 1.4 %fusion.6 = bf16[9,384,256]{2,1,0:T(8,128)(2,1)} fusion(bf16[9,256,128]{2,1,0:T(8,128)(2,1)S(1)} %bitcast.20), kind=kLoop, calls=%fused_computation.8 | loop fusion | flops 7077888 | bytes 2359296 | tf_op jit(solution)/shard_map/concatenate | solution.py:54
  14.3 1.5 %fusion.8 = bf16[9,384,256]{2,1,0:T(8,128)(2,1)} fusion(bf16[9,256,128]{2,1,0:T(8,128)(2,1)S(1)} %bitcast.21), kind=kLoop, calls=%fused_computation.10 | loop fusion | flops 7077888 | bytes 2359296 | tf_op jit(solution)/shard_map/concatenate | solution.py:54
  15.8 1.4 %collective-permute-done.1.ahead_ref = bf16[2,32,4096]{2,1,0:T(8,128)(2,1)S(1)} collective-permute-done((bf16[2,32,4096]{2,1,0:T(8,128)(2,1)}, bf16[2,32,4096]{2,1,0:T(8,128)(2,1)S(1)}, u32[]{:S(2)}, u32[]{:S(2)}) %collective-permute-start.1) | collective-permute-done | bytes 524320 | tf_op jit(solution)/shard_map/ppermute | solution.py:303
  17.2 1.3 %collective-permute-done.back_ref = bf16[2,32,4096]{2,1,0:T(8,128)(2,1)S(1)} collective-permute-done((bf16[2,32,4096]{2,1,0:T(8,128)(2,1)}, bf16[2,32,4096]{2,1,0:T(8,128)(2,1)S(1)}, u32[]{:S(2)}, u32[]{:S(2)}) %collective-permute-start) | collective-permute-done | bytes 524320 | tf_op jit(solution)/shard_map/ppermute | solution.py:302
  19.3 11.2 %first.1 = (bf16[2,32,4096]{2,1,0:T(8,128)(2,1)}, bf16[2,32,4096]{2,1,0:T(8,128)(2,1)}, bf16[2,32,4096]{2,1,0:T(8,128)(2,1)}, bf16[4,32,4224]{2,1,0:T(8,128)(2,1)}) custom-call(s32[1]{0:T(128)} %bitcast.3.flag_ref, bf16[2,32,4096]{2,1,0:T(8,128)(2,1)} %bitcast.28, bf16[2,32,4096]{2,1,0:T(8,128)(2,1)} %copy-done.5, bf16[2,32,4096]{2,1,0:T(8,128)(2,1)} %bitcast.30, ...), custom_call_target="tpu_custom_call" | custom-call | flops 6794772480 | bytes 8815620 | tf_op jit(solution)/shard_map/first/pallas_call | solution.py:267
  30.5 1.3 %collective-permute-start.2 = (bf16[2,32,4096]{2,1,0:T(8,128)(2,1)}, bf16[2,32,4096]{2,1,0:T(8,128)(2,1)S(1)}, u32[]{:S(2)}, u32[]{:S(2)}) collective-permute-start(bf16[2,32,4096]{2,1,0:T(8,128)(2,1)} %get-tuple-element.11.pre_grad_ref), channel_id=1, source_target_pairs={{1,0},{3,2},{5,4},{7,6},{9,8},{11,10},{13,12},{15,14},{17,16},{19,... | collective-permute-start | bytes 1572872 | tf_op jit(solution)/shard_map/ppermute | solution.py:328
  31.8 1.0 %slice.20 = bf16[2,16,4096]{2,1,0:T(8,128)(2,1)S(1)} slice(bf16[2,32,4096]{2,1,0:T(8,128)(2,1)} %get-tuple-element.14), slice={[0:2], [16:32], [0:4096]} | slice | bytes 524288 | tf_op jit(solution)/shard_map/slice | solution.py:284
  32.7 4.6 %collective-permute-start.4 = (bf16[2,16,4096]{2,1,0:T(8,128)(2,1)S(1)}, bf16[2,16,4096]{2,1,0:T(8,128)(2,1)S(1)}, u32[]{:S(2)}, u32[]{:S(2)}) collective-permute-start(bf16[2,16,4096]{2,1,0:T(8,128)(2,1)S(1)} %slice.20), channel_id=1, source_target_pairs={{0,1},{2,3},{4,5},{6,7},{8,9},{10,11},{12,13},{14,15},{16,17},{18,... | collective-permute-start | bytes 786440 | tf_op jit(solution)/shard_map/ppermute | solution.py:284
  37.3 9.4 %sums.1 = bf16[1728,128]{1,0:T(8,128)(2,1)} custom-call(s32[1]{0:T(128)} %bitcast.3.flag_ref, bf16[4,32,4224]{2,1,0:T(8,128)(2,1)} %get-tuple-element.15.act_ref, bf16[2,32,4096]{2,1,0:T(8,128)(2,1)} %get-tuple-element.11.pre_grad_ref, bf16[2,32,4096]{2,1,0:T(8,128)(2,1)} %get-tuple-element.16.middle_ref, bf16[2,32,4096]{2,1,0:T(8,128)(2,1)} %bitcast.26, ...), custom_call_target="tpu_custom_call" | custom-call | flops 6794772480 | bytes 4145156 | tf_op jit(solution)/shard_map/sums/pallas_call | solution.py:267
  46.7 2.0 %reshape.46 = bf16[32,54,128]{2,1,0:T(8,128)(2,1)} reshape(bf16[1728,128]{1,0:T(8,128)(2,1)} %sums.1) | data formatting | bytes 884736 | tf_op jit(solution)/shard_map/reshape | solution.py:350
  48.6 5.9 %all-to-all-start = ((bf16[32,54,128]{2,1,0:T(8,128)(2,1)}), bf16[32,54,128]{2,1,0:T(8,128)(2,1)S(1)}, u32[]{:S(2)}, u32[]{:S(2)}) async-start(bf16[32,54,128]{2,1,0:T(8,128)(2,1)} %reshape.46), calls=%async_computation | async-start | bytes 917504 | tf_op jit(solution)/shard_map/all_to_all | solution.py:349
  55.3 0.8 copy-done.6
  56.1 7.4 %last.1 = (bf16[2,32,4096]{2,1,0:T(8,128)(2,1)}, bf16[2,32,4096]{2,1,0:T(8,128)(2,1)}) custom-call(bf16[2,32,4096]{2,1,0:T(8,128)(2,1)} %bitcast.29, bf16[2,32,4096]{2,1,0:T(8,128)(2,1)} %bitcast.31, bf16[2,32,4096]{2,1,0:T(8,128)(2,1)} %bitcast.35, bf16[2,32,4096]{2,1,0:T(8,128)(2,1)} %get-tuple-element.11.pre_grad_ref, bf16[2,32,4096]{2,1,0:T(8,128)(2,1)} %copy-done.6, ...), custom_call_target="tpu_custom_call" | custom-call | flops 4076863488 | bytes 5439488 | tf_op jit(solution)/shard_map/last/pallas_call | solution.py:267
  63.5 1.0 %slice.18 = bf16[2,16,4096]{2,1,0:T(8,128)(2,1)S(1)} slice(bf16[2,32,4096]{2,1,0:T(8,128)(2,1)} %get-tuple-element.13), slice={[0:2], [16:32], [0:4096]} | slice | bytes 524288 | tf_op jit(solution)/shard_map/slice | solution.py:284
  64.6 3.5 %collective-permute-start.3 = (bf16[2,16,4096]{2,1,0:T(8,128)(2,1)S(1)}, bf16[2,16,4096]{2,1,0:T(8,128)(2,1)S(1)}, u32[]{:S(2)}, u32[]{:S(2)}) collective-permute-start(bf16[2,16,4096]{2,1,0:T(8,128)(2,1)S(1)} %slice.18), channel_id=1, source_target_pairs={{0,1},{2,3},{4,5},{6,7},{8,9},{10,11},{12,13},{14,15},{16,17},{18,... | collective-permute-start | bytes 786440 | tf_op jit(solution)/shard_map/ppermute | solution.py:284
  68.2 0.8 broadcast_in_dim.18
  69.1 4.6 %all-to-all-start.1 = ((bf16[32,54,128]{2,1,0:T(8,128)(2,1)}), bf16[32,54,128]{2,1,0:T(8,128)(2,1)S(1)}, u32[]{:S(2)}, u32[]{:S(2)}) async-start(bf16[32,54,128]{2,1,0:T(8,128)(2,1)} %broadcast_in_dim.18), calls=%async_computation.1 | async-start | bytes 917504 | tf_op jit(solution)/shard_map/all_to_all | solution.py:353
  74.7 12.8 %all-to-all-done.1 = bf16[32,54,128]{2,1,0:T(8,128)(2,1)S(1)} async-done(((bf16[32,54,128]{2,1,0:T(8,128)(2,1)}), bf16[32,54,128]{2,1,0:T(8,128)(2,1)S(1)}, u32[]{:S(2)}, u32[]{:S(2)}) %all-to-all-start.1) | async-done | bytes 442400 | tf_op jit(solution)/shard_map/all_to_all | solution.py:353
  87.6 1.4 %slice_convert_fusion = (f32[3,3,3,64,64]{4,3,2,1,0:T(8,128)}, f32[3,3,3,64,64]{4,3,2,1,0:T(8,128)}) fusion(bf16[3,3,3,64,128]{4,3,2,1,0:T(8,128)(2,1)S(1)} %reshape_reshape.3), kind=kLoop, calls=%fused_computation.23 | loop fusion | flops 221184 | bytes 1327104 | tf_op jit(solution)/shard_map/convert_element_type | solution.py:358
  (29 shorter events, 4.4 us)
Async XLA Ops:
  0.6 9.2 %copy-start.2 = (bf16[3,3,3,64,64]{4,3,2,1,0:T(8,128)(2,1)S(1)}, bf16[3,3,3,64,64]{4,3,2,1,0:T(8,128)(2,1)}, u32[]{:S(2)}) copy-start(bf16[3,3,3,64,64]{4,3,2,1,0:T(8,128)(2,1)} %param.12) | copy-start | bytes 663556
  0.6 16.6 %collective-permute-start.1 = (bf16[2,32,4096]{2,1,0:T(8,128)(2,1)}, bf16[2,32,4096]{2,1,0:T(8,128)(2,1)S(1)}, u32[]{:S(2)}, u32[]{:S(2)}) collective-permute-start(bf16[2,32,4096]{2,1,0:T(8,128)(2,1)} %bitcast.32), channel_id=1, source_target_pairs={{1,0},{3,2},{5,4},{7,6},{9,8},{11,10},{13,12},{15,14},{17,16},{19,... | collective-permute-start | bytes 1572872 | tf_op jit(solution)/shard_map/ppermute | solution.py:303
  2.1 16.4 %collective-permute-start = (bf16[2,32,4096]{2,1,0:T(8,128)(2,1)}, bf16[2,32,4096]{2,1,0:T(8,128)(2,1)S(1)}, u32[]{:S(2)}, u32[]{:S(2)}) collective-permute-start(bf16[2,32,4096]{2,1,0:T(8,128)(2,1)} %bitcast.27), channel_id=1, source_target_pairs={{0,1},{2,3},{4,5},{6,7},{8,9},{10,11},{12,13},{14,15},{16,17},{18,... | collective-permute-start | bytes 1572872 | tf_op jit(solution)/shard_map/ppermute | solution.py:302
  10.1 1.8 %copy-start.3 = (f32[64]{0:T(128)S(1)}, f32[64]{0:T(128)}, u32[]{:S(2)}) copy-start(f32[64]{0:T(128)} %param.11) | copy-start | bytes 772
  17.2 1.3 %copy-start.4 = (bf16[2,32,4096]{2,1,0:T(8,128)(2,1)}, bf16[2,32,4096]{2,1,0:T(8,128)(2,1)S(1)}, u32[]{:S(2)}) copy-start(bf16[2,32,4096]{2,1,0:T(8,128)(2,1)S(1)} %collective-permute-done.1.ahead_ref) | copy-start | bytes 1572868
  18.5 0.8 copy-start.5
  30.5 24.8 %collective-permute-start.2 = (bf16[2,32,4096]{2,1,0:T(8,128)(2,1)}, bf16[2,32,4096]{2,1,0:T(8,128)(2,1)S(1)}, u32[]{:S(2)}, u32[]{:S(2)}) collective-permute-start(bf16[2,32,4096]{2,1,0:T(8,128)(2,1)} %get-tuple-element.11.pre_grad_ref), channel_id=1, source_target_pairs={{1,0},{3,2},{5,4},{7,6},{9,8},{11,10},{13,12},{15,14},{17,16},{19,... | collective-permute-start | bytes 1572872 | tf_op jit(solution)/shard_map/ppermute | solution.py:328
  32.7 21.8 %collective-permute-start.4 = (bf16[2,16,4096]{2,1,0:T(8,128)(2,1)S(1)}, bf16[2,16,4096]{2,1,0:T(8,128)(2,1)S(1)}, u32[]{:S(2)}, u32[]{:S(2)}) collective-permute-start(bf16[2,16,4096]{2,1,0:T(8,128)(2,1)S(1)} %slice.20), channel_id=1, source_target_pairs={{0,1},{2,3},{4,5},{6,7},{8,9},{10,11},{12,13},{14,15},{16,17},{18,... | collective-permute-start | bytes 786440 | tf_op jit(solution)/shard_map/ppermute | solution.py:284
  46.7 7.9 %copy-start = (bf16[2,32,4096]{2,1,0:T(8,128)(2,1)S(1)}, bf16[2,32,4096]{2,1,0:T(8,128)(2,1)}, u32[]{:S(2)}) copy-start(bf16[2,32,4096]{2,1,0:T(8,128)(2,1)} %get-tuple-element.14) | copy-start | bytes 1572868
  48.6 19.5 %all-to-all-start = ((bf16[32,54,128]{2,1,0:T(8,128)(2,1)}), bf16[32,54,128]{2,1,0:T(8,128)(2,1)S(1)}, u32[]{:S(2)}, u32[]{:S(2)}) async-start(bf16[32,54,128]{2,1,0:T(8,128)(2,1)} %reshape.46), calls=%async_computation | async-start | bytes 917504 | tf_op jit(solution)/shard_map/all_to_all | solution.py:349
  55.3 0.8 copy-start.6
  63.5 10.4 %copy-start.1 = (bf16[2,32,4096]{2,1,0:T(8,128)(2,1)S(1)}, bf16[2,32,4096]{2,1,0:T(8,128)(2,1)}, u32[]{:S(2)}) copy-start(bf16[2,32,4096]{2,1,0:T(8,128)(2,1)} %get-tuple-element.13) | copy-start | bytes 1572868
  64.6 9.3 %collective-permute-start.3 = (bf16[2,16,4096]{2,1,0:T(8,128)(2,1)S(1)}, bf16[2,16,4096]{2,1,0:T(8,128)(2,1)S(1)}, u32[]{:S(2)}, u32[]{:S(2)}) collective-permute-start(bf16[2,16,4096]{2,1,0:T(8,128)(2,1)S(1)} %slice.18), channel_id=1, source_target_pairs={{0,1},{2,3},{4,5},{6,7},{8,9},{10,11},{12,13},{14,15},{16,17},{18,... | collective-permute-start | bytes 786440 | tf_op jit(solution)/shard_map/ppermute | solution.py:284
  69.1 18.4 %all-to-all-start.1 = ((bf16[32,54,128]{2,1,0:T(8,128)(2,1)}), bf16[32,54,128]{2,1,0:T(8,128)(2,1)S(1)}, u32[]{:S(2)}, u32[]{:S(2)}) async-start(bf16[32,54,128]{2,1,0:T(8,128)(2,1)} %broadcast_in_dim.18), calls=%async_computation.1 | async-start | bytes 917504 | tf_op jit(solution)/shard_map/all_to_all | solution.py:353

commit v2 on v1

v2 whole, which is shorter than its diff:
```python
import functools
import math

import jax
import jax.numpy as jnp
from jax import lax
from jax.experimental import pallas as pl
from jax.experimental.pallas import tpu as pltpu
from jax.sharding import Mesh, PartitionSpec as P

F32 = jnp.float32
BF16 = jnp.bfloat16
OUT = 256
WIN = 384
VMEM = pl.BlockSpec(memory_space=pltpu.VMEM)
SMEM = pl.BlockSpec(memory_space=pltpu.SMEM)


def logistic(value):
    return 1.0 / (1.0 + jnp.exp(-value))


def slope_of(value):
    s = logistic(value)
    return s * (1.0 + value * (1.0 - s))


def row_shifts(value):
    rows = value.shape[0]
    row = lax.broadcasted_iota(jnp.int32, value.shape, 0)
    down = jnp.where(row == 0, 0.0, pltpu.roll(value, 1, axis=0))
    up = jnp.where(row == rows - 1, 0.0, pltpu.roll(value, rows - 1, axis=0))
    return down, value, up


def column_shift(value, chans):
    pad = jnp.zeros((value.shape[0], 2 * chans), value.dtype)
    return pltpu.roll(jnp.concatenate([value, pad], axis=1), chans, axis=1)


def put_shifted(ref, frame, value, chans):
    for k, part in enumerate(row_shifts(column_shift(value, chans))):
        ref[frame, k] = part.astype(BF16)


def spread(weight_ref, tap):
    chans = weight_ref.shape[1]
    zero = jnp.zeros((chans, chans), F32)
    left = [
        jnp.concatenate([weight_ref[3 * tap + kq].astype(F32), zero], axis=1) for kq in range(3)
    ]
    right = [pltpu.roll(value, chans, axis=1) for value in left]
    return left, right


def band_forward(weight_ref, out_ref):
    chans = weight_ref.shape[1]
    half = 2 * chans
    for tap in range(9):
        left, right = spread(weight_ref, tap)
        pairs = [left[0], left[1] + right[0], left[2] + right[1], right[2]]
        at = tap * WIN
        for c, pair in enumerate(pairs):
            pair = pair.astype(BF16)
            out_ref[at + chans * c : at + chans * (c + 1), :half] = pair
            out_ref[at + half + chans * c : at + half + chans * (c + 1), half:] = pair
        zero = jnp.zeros((half, half), BF16)
        out_ref[at + OUT : at + WIN, :half] = zero
        out_ref[at : at + half, half:] = zero


def band_turned(weight_ref, out_ref):
    chans = weight_ref.shape[1]
    half = 2 * chans
    zero = jnp.zeros((chans, half), BF16)
    for tap in range(9):
        left, right = spread(weight_ref, 8 - tap)
        even = ((left[2] + right[1]).astype(BF16), left[0].astype(BF16))
        odd = (right[2].astype(BF16), (left[1] + right[0]).astype(BF16))
        at = tap * WIN
        for d, tiles in enumerate((even + (zero,), odd + (zero,), (zero,) + even, (zero,) + odd)):
            for m, tile in enumerate(tiles):
                out_ref[chans * d : chans * (d + 1), at + half * m : at + half * (m + 1)] = tile


def conv(frame_of, weight_ref, taps, turned=False):
    pieces = []
    for kt in taps:
        ref, frame = frame_of(kt)
        groups = ref.shape[3] // OUT
        for kr in range(3):
            pieces.append(
                jnp.concatenate(
                    [ref[frame, kr, :, OUT * j : OUT * j + WIN] for j in range(groups)], axis=0
                )
            )
    lhs = jnp.concatenate(pieces, axis=1)
    span = slice(taps[0] * 3 * WIN, (taps[-1] + 1) * 3 * WIN)
    if turned:
        return lax.dot_general(
            lhs, weight_ref[:, span], (((1,), (1,)), ((), ())), preferred_element_type=F32
        )
    return jnp.dot(lhs, weight_ref[span, :], preferred_element_type=F32)


def silu(value):
    value = value.astype(F32)
    return (value * logistic(value)).astype(BF16).astype(F32)


def put_rows(ref, frame, value):
    for k, part in enumerate(row_shifts(value)):
        ref[frame, 2 - k] = part.astype(BF16)


def put_groups(ref, frame, value):
    rows = ref.shape[1]
    for j in range(ref.shape[2] // OUT):
        ref[frame, :, OUT * j : OUT * (j + 1)] = value[rows * j : rows * (j + 1)]


def own_kernel(
    place_ref,
    stack_ref,
    input_cache_ref,
    weight_ref,
    band_first_ref,
    band_second_ref,
    act_ref,
    cot_cols_ref,
    cot_rows_ref,
    pre_ref,
    grad_ref,
    cache_grad_ref,
    cache_sum_ref,
    cache_ref,
):
    frames, chans = cot_cols_ref.shape[0], weight_ref.shape[1]
    w_first_ref, w_second_ref = weight_ref.at[:27], weight_ref.at[27:]
    band_forward(w_first_ref, band_first_ref)
    band_turned(w_second_ref, band_second_ref)
    first = place_ref[0] == 0

    @pl.loop(0, frames)
    def _(f):
        put_shifted(act_ref, f + 2, silu(stack_ref[f]), chans)
        value = stack_ref[frames + f].astype(F32)
        put_shifted(cot_cols_ref, f, value, chans)
        put_rows(cot_rows_ref, f, value)

    @pl.loop(0, 2)
    def _(f):
        value = jnp.where(first, stack_ref[2 * frames + f].astype(F32), 0.0)
        cache_ref[f] = column_shift(value, chans).astype(BF16)

    for f in range(frames):
        taps = tuple(kt for kt in range(3) if f + kt >= 2)
        pre_ref[f] = conv(lambda kt: (act_ref, f + kt), band_first_ref, taps)
        taps = tuple(kt for kt in range(3) if f + kt < frames)
        grad_ref[f] = conv(lambda kt: (cot_cols_ref, f + kt), band_second_ref, taps, True)

    @pl.when(first)
    def _():
        @pl.loop(0, 2)
        def _(f):
            put_shifted(act_ref, f, silu(input_cache_ref[f]), chans)

        for f in range(min(2, frames)):
            taps = tuple(kt for kt in range(3) if f + kt < 2)
            pre_ref[f] += conv(lambda kt: (act_ref, f + kt), band_first_ref, taps)

    for f in range(2):
        taps = (1, 2) if f else (2,)
        grad = conv(lambda kt: (cot_cols_ref, f + kt - 2), band_second_ref, taps, True)
        put_groups(cache_grad_ref, f, grad.astype(BF16))
    for kt in range(2):
        cache_sum_ref[kt] = correlate(
            [(cache_ref, (a,)) for a in range(kt, 2)],
            [(cot_rows_ref, a - kt) for a in range(kt, 2)],
        )


def halo_kernel(
    place_ref,
    halo_ref,
    bias_ref,
    band_first_ref,
    band_second_ref,
    act_own_ref,
    pre_ref,
    grad_ref,
    pre_grad_ref,
    act_ref,
    middle_ref,
    cot_rows_ref,
    grad_rows_ref,
    shifted,
    pre_total,
    grad_total,
    flat,
):
    frames, chans = pre_ref.shape[0], OUT // 4
    first, end = place_ref[0] == 0, place_ref[0] == place_ref[1] - 1
    ahead = halo_ref.shape[0] - 2
    pre_total[...] = pre_ref[...]
    grad_total[...] = grad_ref[...]

    @pl.when(first)
    def _():
        for f in range(2):
            act_ref[f] = act_own_ref[f, 1]

    @pl.when(jnp.logical_not(first))
    def _():
        @pl.loop(0, 2)
        def _(f):
            put_shifted(shifted, f, silu(halo_ref[f]), chans)
            act_ref[f] = shifted[f, 1]

        for f in range(min(2, frames)):
            taps = tuple(kt for kt in range(3) if f + kt < 2)
            pre_total[f] += conv(lambda kt: (shifted, f + kt), band_first_ref, taps)

    @pl.when(end)
    def _():
        cot_rows_ref[...] = jnp.zeros(cot_rows_ref.shape, BF16)

    @pl.when(jnp.logical_not(end))
    def _():
        @pl.loop(0, 2)
        def _(f):
            value = halo_ref[ahead + f].astype(F32)
            put_shifted(shifted, f, value, chans)
            put_rows(cot_rows_ref, f, value)

        for f in range(max(0, frames - 2), frames):
            taps = tuple(kt for kt in range(3) if f + kt >= frames)
            grad_total[f] += conv(
                lambda kt: (shifted, f + kt - frames), band_second_ref, taps, True
            )

    bias = jnp.concatenate([bias_ref[...], jnp.zeros((1, chans), F32)], axis=1)
    bias = bias + pltpu.roll(bias, chans, axis=1)
    bias = jnp.concatenate([bias] * (OUT // (2 * chans)), axis=1)

    @pl.loop(0, frames)
    def _(f):
        pre, grad = pre_total[f] + bias, grad_total[f]
        s = logistic(pre)
        put_groups(pre_grad_ref, f, (grad * (s * (1.0 + pre * (1.0 - s)))).astype(BF16))
        put_groups(flat, 0, pre * s)
        middle_ref[f] = column_shift(flat[0], chans).astype(BF16)
        put_rows(grad_rows_ref, f, pre_grad_ref[f].astype(F32))


def correlate(sources, upstreams):
    groups = upstreams[0][0].shape[3] // OUT
    left = jnp.concatenate(
        [
            ref[at + (slice(None), slice(OUT * j, OUT * j + WIN))]
            for ref, at in sources
            for j in range(groups)
        ],
        axis=0,
    )
    right = jnp.concatenate(
        [
            jnp.concatenate(
                [
                    ref[t, k, :, OUT * j : OUT * (j + 1)]
                    for ref, t in upstreams
                    for j in range(groups)
                ],
                axis=0,
            )
            for k in range(3)
        ],
        axis=1,
    )
    return lax.dot_general(
        left, right, (((0,), (0,)), ((), ())), preferred_element_type=F32
    )


def sums_kernel(
    act_ref,
    act_back_ref,
    middle_ref,
    cot_ref,
    cot_ahead_ref,
    grad_ref,
    cache_sum_ref,
    out_ref,
    total_first,
    total_second,
):
    frames = middle_ref.shape[0]
    chans = OUT // 4
    lane = lax.broadcasted_iota(jnp.int32, (chans, 2 * chans), 1) < chans

    def tap(total, kr, kq):
        cut = lambda d: total[
            chans * (kq + d) : chans * (kq + d + 1),
            OUT * kr + 2 * chans * (d // 2) : OUT * kr + 2 * chans * (d // 2 + 1),
        ]
        value = jnp.where(lane, cut(0) + cut(2), cut(1) + cut(3))
        return value + pltpu.roll(value, chans, axis=1)

    acts = [(act_back_ref, (f,)) for f in range(2)]
    acts += [(act_ref, (f + 2, 1)) for f in range(frames)]
    mids = [(middle_ref, (f,)) for f in range(frames)]
    cots = [(cot_ref, f) for f in range(frames)] + [(cot_ahead_ref, f) for f in range(2)]
    grads = [(grad_ref, f) for f in range(frames)]
    used, whole = 27 * chans, out_ref.shape[0]
    for kt in range(3):
        total_first[...] = correlate(acts[kt : kt + frames], grads)
        second = correlate(mids, cots[2 - kt : 2 - kt + frames])
        total_second[...] = second + cache_sum_ref[kt] if kt < 2 else second
        for kr in range(3):
            for kq in range(3):
                at = ((kt * 3 + kr) * 3 + kq) * chans
                out_ref[at : at + chans, :] = jnp.where(
                    lane, tap(total_first, kr, kq), tap(total_second, kr, kq)
                ).astype(BF16)
    if whole > used:
        out_ref[used:, :] = jnp.zeros((whole - used, 2 * chans), BF16)


def share_kernel(factor, parts_ref, out_ref):
    total = parts_ref[0].astype(F32)
    for k in range(1, parts_ref.shape[0]):
        total = total + parts_ref[k].astype(F32)
    total = (total * factor).astype(BF16)
    for k in range(out_ref.shape[0]):
        out_ref[k] = total


def last_kernel(
    stack_ref,
    cache_ref,
    pre_grad_ref,
    ahead_ref,
    weight_ref,
    input_grad_ref,
    cache_grad_ref,
    shifted,
    band,
):
    frames, rows, lanes = pre_grad_ref.shape
    chans = weight_ref.shape[1]
    groups = lanes // OUT
    band_turned(weight_ref, band)

    @pl.loop(0, frames)
    def _(f):
        put_shifted(shifted, f, pre_grad_ref[f].astype(F32), chans)

    @pl.loop(0, 2)
    def _(f):
        put_shifted(shifted, f + frames, ahead_ref[f].astype(F32), chans)

    @pl.loop(0, frames)
    def _(f):
        grad = conv(lambda kt: (shifted, f + kt), band, (0, 1, 2), True)
        for j in range(groups):
            cut = slice(OUT * j, OUT * (j + 1))
            value = grad[rows * j : rows * (j + 1)] * slope_of(stack_ref[f, :, cut].astype(F32))
            cot = stack_ref[frames + f, :, cut].astype(F32)
            input_grad_ref[f, :, cut] = (cot + value).astype(BF16)

    for f in range(2):
        grad = conv(lambda kt: (shifted, f + kt - 2), band, (1, 2) if f else (2,), True)
        for j in range(groups):
            cut = slice(OUT * j, OUT * (j + 1))
            value = grad[rows * j : rows * (j + 1)] * slope_of(cache_ref[f, :, cut].astype(F32))
            cache_grad_ref[f, :, cut] = value.astype(BF16)


def call(kernel, name, out_shape, scratch, flops, args, limit=20):
    smem = [a.dtype == jnp.int32 for a in args]
    moved = sum(a.size * a.dtype.itemsize for a in args)
    moved += sum(o.size * o.dtype.itemsize for o in jax.tree.leaves(out_shape))
    return pl.pallas_call(
        kernel,
        out_shape=out_shape,
        in_specs=[SMEM if s else VMEM for s in smem],
        out_specs=jax.tree.map(lambda _: VMEM, out_shape),
        scratch_shapes=scratch,
        compiler_params=pltpu.CompilerParams(vmem_limit_bytes=limit * 1024 * 1024),
        cost_estimate=pl.CostEstimate(flops=flops, bytes_accessed=moved, transcendentals=0),
        name=name,
    )(*args)


def to_row_parts(grads, count):
    rows = grads.shape[1] // count
    mine = grads[:, :rows]
    place = lax.axis_index("tm")
    for k in range(1, count):
        part = lax.ppermute(grads[:, k * rows : (k + 1) * rows], "tm", [(0, k)])
        mine = jnp.where(place == k, part, mine)
    return mine


def body(
    block_input, input_cache, middle_cache, first_weight, first_bias, second_weight, cotangent
):
    chans = first_weight.shape[3]
    tm, chips, cores = (lax.axis_size(axis) for axis in ("tm", "chip", "core"))
    clips = chips * cores
    _, frames, rows, lanes = block_input.shape
    width = lanes // chans
    factor = 1.0 / math.sqrt(block_input.shape[0] * clips * frames * tm * rows * width)
    x, cot = block_input[0], cotangent[0]
    icache, mcache = input_cache[0], middle_cache[0]
    w_first = first_weight.reshape(27, chans, chans)
    w_second = second_weight.reshape(27, chans, chans)
    index = lax.axis_index("tm").astype(jnp.int32)
    core = lax.axis_index("core").astype(jnp.int32)
    place = jnp.stack([index, jnp.int32(tm)])
    onward = [(i, i + 1) for i in range(tm - 1)]
    backward = [(i + 1, i) for i in range(tm - 1)]
    if tm == 2:
        sent = jnp.where(index == 0, x[frames - 2 :], cot[:2])
        halo = lax.ppermute(sent, "tm", onward + backward)
    else:
        back = lax.ppermute(x[frames - 2 :], "tm", onward)
        halo = jnp.concatenate([back, lax.ppermute(cot[:2], "tm", backward)])

    stack, weights = jnp.concatenate([x, cot, mcache]), jnp.concatenate([w_first, w_second])
    padded = lanes + 2 * chans
    make = lambda *s, t=BF16: jax.ShapeDtypeStruct(s, t)
    tap_flops = 2 * rows * width * 9 * chans * chans * 3
    positions = rows * lanes // OUT
    (
        band_first,
        band_second,
        act,
        cot_cols,
        cot_rows,
        pre,
        grad,
        mid_cache_grad,
        cache_sum,
    ) = call(
        own_kernel,
        "own",
        (
            make(9 * WIN, OUT),
            make(OUT, 9 * WIN),
            make(frames + 2, 3, rows, padded),
            make(frames, 3, rows, padded),
            make(frames, 3, rows, lanes),
            make(frames, positions, OUT, t=F32),
            make(frames, positions, OUT, t=F32),
            make(2, rows, lanes),
            make(2, WIN, 3 * OUT, t=F32),
        ),
        [
            pltpu.VMEM((2, rows, padded), BF16),
        ],
        tap_flops * 12,
        (
            place,
            stack,
            icache,
            weights,
        ),
    )
    pre_grad, act_back, middle, cot_ahead, grad_rows = call(
        halo_kernel,
        "halo",
        (
            make(frames, rows, lanes),
            make(2, rows, padded),
            make(frames, rows, padded),
            make(2, 3, rows, lanes),
            make(frames, 3, rows, lanes),
        ),
        [
            pltpu.VMEM((2, 3, rows, padded), BF16),
            pltpu.VMEM((frames, positions, OUT), F32),
            pltpu.VMEM((frames, positions, OUT), F32),
            pltpu.VMEM((1, rows, lanes), F32),
        ],
        tap_flops * 6,
        (
            place,
            halo,
            first_bias.reshape(1, chans),
            band_first,
            band_second,
            act,
            pre,
            grad,
        ),
    )
    grad_ahead = lax.ppermute(pre_grad[:2], "tm", backward)
    count = clips * tm
    share = -(-27 * chans // (8 * count)) * 8
    sums = call(
        sums_kernel,
        "sums",
        make(count * share, 2 * chans),
        [pltpu.VMEM((WIN, 3 * OUT), F32), pltpu.VMEM((WIN, 3 * OUT), F32)],
        tap_flops * 12,
        (act, act_back, middle, cot_rows, cot_ahead, grad_rows, cache_sum),
    )
    parts = lax.all_to_all(
        sums.reshape(count, share, 2 * chans), ("core", "chip", "tm"), 0, 0, tiled=True
    )
    shares = call(
        functools.partial(share_kernel, factor),
        "share",
        make(count // cores, share, 2 * chans),
        [],
        count * share * 2 * chans,
        (parts,),
        limit=60,
    )
    whole = lax.all_to_all(shares, ("chip", "tm"), 0, 0, tiled=True)
    whole = whole.reshape(count // cores * share, 2 * chans)
    if cores == 2:
        other = lax.ppermute(whole, "core", [(0, 1), (1, 0)])
        low, high = jnp.where(core == 0, whole, other), jnp.where(core == 0, other, whole)
        whole = jnp.concatenate([low, high])
    whole = whole[: 27 * chans].reshape(3, 3, 3, chans, 2 * chans)
    first_total = whole[..., :chans].astype(F32)
    second_total = whole[..., chans:].astype(F32)

    input_grad, in_cache_grad = call(
        last_kernel,
        "last",
        (make(frames, rows, lanes), make(2, rows, lanes)),
        [pltpu.VMEM((frames + 2, 3, rows, padded), BF16), pltpu.VMEM((OUT, 9 * WIN), BF16)],
        tap_flops * 9,
        (stack, icache, pre_grad, grad_ahead, weights),
    )
    cache_grads = to_row_parts(jnp.concatenate([in_cache_grad, mid_cache_grad]), tm)
    return (
        input_grad[None],
        cache_grads[None, :2],
        cache_grads[None, 2:],
        first_total,
        second_total,
    )


def solution(mesh):
    clips, tm = mesh.devices.shape
    cores = 2 if clips % 2 == 0 else 1
    split = Mesh(mesh.devices.reshape(clips // cores, cores, tm), ("chip", "core", "tm"))
    clip = ("chip", "core")
    return jax.shard_map(
        body,
        mesh=split,
        in_specs=(
            P(clip, "tm", None, None),
            P(clip, None, None, None),
            P(clip, None, None, None),
            P(),
            P(),
            P(),
            P(clip, "tm", None, None),
        ),
        out_specs=(
            P(clip, "tm", None, None),
            P(clip, None, "tm", None),
            P(clip, None, "tm", None),
            P(),
            P(),
        ),
        check_vma=False,
    )
```

time: 90 us -> 68.4 us (0.76)
  starting transfers between devices: 26.3 us -> 18.5 us
  local copies, waits for them, and re-layouts: 8.74 us -> 1.74 us
  other arithmetic: 9.42 us -> 3.4 us
  Pallas kernels: 27.9 us -> 25.7 us
  waiting for transfers between devices: 15.8 us -> 17.8 us
    ppermute x4 -> x3, starting transfers between devices: 14.5 us -> 5.6 us  [the longest x1 3.06 us: body(): halo = lax.ppermute(sent, 'tm', onward + backward)]
    concatenate x6 -> x3, other arithmetic: 6.43 us -> 0.38 us  [the longest x1 0.17 us: body(): jnp.concatenate([w_first, w_second])]
    unnamed x16 -> x15, local copies, waits for them, and re-layouts: 3.11 us -> 0.84 us
    pallas_call x3 -> x5, Pallas kernels: 27.9 us -> 25.7 us  [call(): pl.pallas_call(kernel, out_shape=out_shape, in_specs=[SMEM if s else VMEM...]
    slice x2 -> x1, local copies, waits for them, and re-layouts: 2.01 us -> 0.04 us  [to_row_parts(): part = lax.ppermute(grads[:, k * rows:(k + 1) * rows], 'tm', [(0, k)])]
    reshape x1 -> x0, local copies, waits for them, and re-layouts: 1.96 us -> none  [body(): padded_sums.reshape(count, share, 2 * chans)]
    select_n x0 -> x3, other arithmetic: none -> 1.51 us  [the longest x1 1.41 us: body(): sent = jnp.where(index == 0, x[frames - 2:], cot[:2])]
    broadcast_in_dim x2 -> x0, other arithmetic: 1.46 us -> none  [to_row_parts(): return mine[None]]
  transfers between devices with their start and end apart: 7 -> 6, of which waited for: 4 -> 6; matrix products, arithmetic and copies ran while one was open for 17% -> 2% of each run, Pallas kernels for 19% -> 32%
where the time goes in v2:
time: 68.4 us; the launch traced here: 68 us
  Pallas kernels  25.7 us (38%)
  starting transfers between devices  18.5 us (27%)
  waiting for transfers between devices  17.8 us (26%)
  other arithmetic  3.4 us (5%)
  local copies, waits for them, and re-layouts  1.74 us (3%)
  between operations  0.82 us (1%)
    pallas_call x5, Pallas kernels, call(): pl.pallas_call(kernel, out_shape=out_shape, in_specs=[SMEM if s else VMEM...  25.7 us
    all_to_all x1, starting transfers between devices, body(): lax.all_to_all(sums.reshape(count, share, 2 * chans), ('core', 'chip', 't...  7.91 us
    all_to_all x1, waiting for transfers between devices, body(): whole = lax.all_to_all(shares, ('chip', 'tm'), 0, 0, tiled=True)  6.83 us
    all_to_all x1, waiting for transfers between devices, body(): lax.all_to_all(sums.reshape(count, share, 2 * chans), ('core', 'chip', 't...  5.69 us
    all_to_all x1, starting transfers between devices, body(): whole = lax.all_to_all(shares, ('chip', 'tm'), 0, 0, tiled=True)  3.53 us
    ppermute x1, starting transfers between devices, body(): halo = lax.ppermute(sent, 'tm', onward + backward)  3.06 us
    ppermute x1, starting transfers between devices, to_row_parts(): part = lax.ppermute(grads[:, k * rows:(k + 1) * rows], 'tm', [(0, k)])  2.54 us
    ppermute x1, waiting for transfers between devices, to_row_parts(): part = lax.ppermute(grads[:, k * rows:(k + 1) * rows], 'tm', [(0, k)])  2.12 us
  transfers between devices with their start and end apart: 6, of which 6 were waited for; matrix products, arithmetic and copies ran while one was open for 2% of the time, Pallas kernels for 32%

profile of v2, /device:TPU:0, one launch (start us, length us, event | category | flops | bytes accessed | tf_op | source)
XLA Modules:
  0.0 68.0 jit_solution(15396618679073321154)
XLA Ops:
  0.7 1.4 %broadcast_select_fusion = bf16[2,32,4096]{2,1,0:T(8,128)(2,1)S(1)} fusion(pred[]{:T(512)S(6)} %eq.10, bf16[1,2,32,4096]{3,2,1,0:T(8,128)(2,1)} %param.13, bf16[1,2,32,4096]{3,2,1,0:T(8,128)(2,1)} %param.7), kind=kLoop, calls=%fused_computation.3 | loop fusion | flops 262144 | bytes 1572865 | tf_op jit(solution)/shard_map/jit(_where)/select_n | solution.py:424
  2.1 3.1 %collective-permute-start = (bf16[2,32,4096]{2,1,0:T(8,128)(2,1)S(1)}, bf16[2,32,4096]{2,1,0:T(8,128)(2,1)S(1)}, u32[]{:S(2)}, u32[]{:S(2)}) collective-permute-start(bf16[2,32,4096]{2,1,0:T(8,128)(2,1)S(1)} %broadcast_select_fusion), channel_id=1, source_target_pairs={{0,1},{1,0},{2,3},{3,2},{4,5},{5,4},{6,7},{7,6},{8,9},{9,8},{10,11... | collective-permute-start | bytes 1572872 | tf_op jit(solution)/shard_map/ppermute | solution.py:425
  5.2 0.2 pad_maximum_fusion.1.weight_ref
  5.4 0.2 pad_maximum_fusion.stack_ref
  5.6 0.1 pad_add_fusion.place_ref
  5.6 0.8 %copy-done = bf16[1,2,32,4096]{3,2,1,0:T(8,128)(2,1)S(1)} copy-done((bf16[1,2,32,4096]{3,2,1,0:T(8,128)(2,1)S(1)}, bf16[1,2,32,4096]{3,2,1,0:T(8,128)(2,1)}, u32[]{:S(2)}) %copy-start) | copy-done | bytes 524312
  6.4 9.3 %own.1 = (bf16[3456,256]{1,0:T(8,128)(2,1)S(1)}, bf16[256,3456]{1,0:T(8,128)(2,1)S(1)}, bf16[4,3,32,4224]{3,2,1,0:T(8,128)(2,1)S(1)}, bf16[2,3,32,4224]{3,2,1,0:...) custom-call(s32[2]{0:T(128)S(1)} %pad_add_fusion.place_ref, ...), custom_call_target="tpu_custom_call" | custom-call | flops 5435817984 | bytes 17498120 | tf_op jit(solution)/shard_map/own/pallas_call | solution.py:383
  15.7 1.4 %collective-permute-done.halo_ref = bf16[2,32,4096]{2,1,0:T(8,128)(2,1)S(1)} collective-permute-done((bf16[2,32,4096]{2,1,0:T(8,128)(2,1)S(1)}, bf16[2,32,4096]{2,1,0:T(8,128)(2,1)S(1)}, u32[]{:S(2)}, u32[]{:S(2)}) %collective-permute-start) | collective-permute-done | bytes 524320 | tf_op jit(solution)/shard_map/ppermute | solution.py:425
  17.1 4.0 %halo.1 = (bf16[2,32,4096]{2,1,0:T(8,128)(2,1)}, bf16[2,32,4224]{2,1,0:T(8,128)(2,1)S(1)}, bf16[2,32,4224]{2,1,0:T(8,128)(2,1)S(1)}, bf16[2,3,32,4096]{3,2,1,0:T(8,128)(2,1)S(1)}, bf16[2,3,32,4096]{3,2,1,0:T(8,128)(2,1)S(1)}) custom-call(s32[2]{0:T(128)S(1)} %pad_add_fusion.place_ref, bf16[2,32,4096]{2,1,0:T(8,128)(2,1)S(1)} %collective-permute-done.halo_ref, ...), custom_call_target="tpu_custom_call" | custom-call | flops 2717908992 | bytes 14156040 | tf_op jit(solution)/shard_map/halo/pallas_call | solution.py:383
  21.1 1.5 %collective-permute-start.1 = (bf16[2,32,4096]{2,1,0:T(8,128)(2,1)}, bf16[2,32,4096]{2,1,0:T(8,128)(2,1)}, u32[]{:S(2)}, u32[]{:S(2)}) collective-permute-start(bf16[2,32,4096]{2,1,0:T(8,128)(2,1)} %get-tuple-element.25.pre_grad_ref), channel_id=1, source_target_pairs={{1,0},{3,2},{5,4},{7,6},{9,8},{11,10},{13,12},{15,14},{17,16},{19,... | collective-permute-start | bytes 1572872 | tf_op jit(solution)/shard_map/ppermute | solution.py:498
  22.6 4.8 %sums.1 = bf16[1792,128]{1,0:T(8,128)(2,1)} custom-call(bf16[4,3,32,4224]{3,2,1,0:T(8,128)(2,1)S(1)} %get-tuple-element.22.act_own_ref.act_ref, bf16[2,32,4224]{2,1,0:T(8,128)(2,1)S(1)} %get-tuple-element.29.act_back_ref, bf16[2,32,4224]{2,1,0:T(8,128)(2,1)S(1)} %get-tuple-element.30.middle_ref, bf16[2,3,32,4096]{3,2,1,0:T(8,128)(2,1)S(1)} %get-tuple-element.31.cot_ref, ...), custom_call_target="tpu_custom_call" | custom-call | flops 5435817984 | bytes 11862016 | tf_op jit(solution)/shard_map/sums/pallas_call | solution.py:383
  27.4 7.9 %all-to-all-start = ((bf16[32,56,128]{2,1,0:T(8,128)(2,1)}), bf16[32,56,128]{2,1,0:T(8,128)(2,1)}, u32[]{:S(2)}, u32[]{:S(2)}) async-start(bf16[32,56,128]{2,1,0:T(8,128)(2,1)} %bitcast.11), calls=%async_computation | async-start | bytes 917504 | tf_op jit(solution)/shard_map/all_to_all | solution.py:509
  35.3 1.1 %collective-permute-done.1.ahead_ref = bf16[2,32,4096]{2,1,0:T(8,128)(2,1)} collective-permute-done((bf16[2,32,4096]{2,1,0:T(8,128)(2,1)}, bf16[2,32,4096]{2,1,0:T(8,128)(2,1)}, u32[]{:S(2)}, u32[]{:S(2)}) %collective-permute-start.1) | collective-permute-done | bytes 524320 | tf_op jit(solution)/shard_map/ppermute | solution.py:498
  36.4 5.9 %last.1 = (bf16[2,32,4096]{2,1,0:T(8,128)(2,1)}, bf16[2,32,4096]{2,1,0:T(8,128)(2,1)S(1)}) custom-call(bf16[6,32,4096]{2,1,0:T(8,128)(2,1)S(1)} %pad_maximum_fusion.stack_ref, bf16[2,32,4096]{2,1,0:T(8,128)(2,1)S(1)} %bitcast.21, bf16[2,32,4096]{2,1,0:T(8,128)(2,1)} %get-tuple-element.25.pre_grad_ref, bf16[2,32,4096]{2,1,0:T(8,128)(2,1)} %collective-permute-done.1.ahead_ref, ...), custom_call_target="tpu_custom_call" | custom-call | flops 4076863488 | bytes 4636672 | tf_op jit(solution)/shard_map/last/pallas_call | solution.py:383
  42.4 2.5 %collective-permute-start.2 = (bf16[4,16,4096]{2,1,0:T(8,128)(2,1)S(1)}, bf16[4,16,4096]{2,1,0:T(8,128)(2,1)S(1)}, u32[]{:S(2)}, u32[]{:S(2)}) collective-permute-start(bf16[4,16,4096]{2,1,0:T(8,128)(2,1)S(1)} %slice.28), channel_id=1, source_target_pairs={{0,1},{2,3},{4,5},{6,7},{8,9},{10,11},{12,13},{14,15},{16,17},{18,... | collective-permute-start | bytes 1572872 | tf_op jit(solution)/shard_map/ppermute | solution.py:400
  45.0 5.7 %all-to-all-done.parts_ref = bf16[32,56,128]{2,1,0:T(8,128)(2,1)} async-done(((bf16[32,56,128]{2,1,0:T(8,128)(2,1)}), bf16[32,56,128]{2,1,0:T(8,128)(2,1)}, u32[]{:S(2)}, u32[]{:S(2)}) %all-to-all-start) | async-done | bytes 458784 | tf_op jit(solution)/shard_map/all_to_all | solution.py:509
  50.7 1.8 %share.1 = bf16[16,56,128]{2,1,0:T(8,128)(2,1)} custom-call(bf16[32,56,128]{2,1,0:T(8,128)(2,1)} %all-to-all-done.parts_ref), custom_call_target="tpu_custom_call" | custom-call | flops 229376 | bytes 688128 | tf_op jit(solution)/shard_map/share/pallas_call | solution.py:383
  52.5 3.5 %all-to-all-start.1 = ((bf16[16,56,128]{2,1,0:T(8,128)(2,1)}), bf16[16,56,128]{2,1,0:T(8,128)(2,1)S(1)}, u32[]{:S(2)}, u32[]{:S(2)}) async-start(bf16[16,56,128]{2,1,0:T(8,128)(2,1)} %share.1), calls=%async_computation.1 | async-start | bytes 458752 | tf_op jit(solution)/shard_map/all_to_all | solution.py:521
  56.0 2.1 %collective-permute-done.2 = bf16[4,16,4096]{2,1,0:T(8,128)(2,1)S(1)} collective-permute-done((bf16[4,16,4096]{2,1,0:T(8,128)(2,1)S(1)}, bf16[4,16,4096]{2,1,0:T(8,128)(2,1)S(1)}, u32[]{:S(2)}, u32[]{:S(2)}) %collective-permute-start.2) | collective-permute-done | bytes 524320 | tf_op jit(solution)/shard_map/ppermute | solution.py:400
  58.1 0.1 slice_select_fusion
  58.2 6.8 %all-to-all-done.1 = bf16[16,56,128]{2,1,0:T(8,128)(2,1)S(1)} async-done(((bf16[16,56,128]{2,1,0:T(8,128)(2,1)}), bf16[16,56,128]{2,1,0:T(8,128)(2,1)S(1)}, u32[]{:S(2)}, u32[]{:S(2)}) %all-to-all-start.1) | async-done | bytes 229408 | tf_op jit(solution)/shard_map/all_to_all | solution.py:521
  65.0 0.8 %slice_bitcast_fusion = (bf16[1,2,16,4096]{3,2,1,0:T(8,128)(2,1)}, bf16[1,2,16,4096]{3,2,1,0:T(8,128)(2,1)}) fusion(bf16[4,16,4096]{2,1,0:T(8,128)(2,1)S(1)} %slice_select_fusion), kind=kLoop, calls=%fused_computation.7 | loop fusion | bytes 1048576 | tf_op jit(solution)/shard_map/broadcast_in_dim | solution.py:543
  65.8 0.7 collective-permute-done.3
  66.6 1.4 %slice_convert_fusion = (f32[3,3,3,64,64]{4,3,2,1,0:T(8,128)}, f32[3,3,3,64,64]{4,3,2,1,0:T(8,128)}) fusion(bf16[3,3,3,64,128]{4,3,2,1,0:T(8,128)(2,1)S(1)} %bitcast.23), kind=kLoop, calls=%fused_computation.4 | loop fusion | flops 221184 | bytes 1327104 | tf_op jit(solution)/shard_map/convert_element_type | solution.py:529
  (19 shorter events, 0.2 us)
Async XLA Ops:
  0.6 4.5 %copy-start.5 = (bf16[3,3,3,64,64]{4,3,2,1,0:T(8,128)(2,1)S(1)}, bf16[3,3,3,64,64]{4,3,2,1,0:T(8,128)(2,1)}, u32[]{:S(2)}) copy-start(bf16[3,3,3,64,64]{4,3,2,1,0:T(8,128)(2,1)} %param.12) | copy-start | bytes 663556
  0.6 4.5 %copy-start.6 = (bf16[3,3,3,64,64]{4,3,2,1,0:T(8,128)(2,1)S(1)}, bf16[3,3,3,64,64]{4,3,2,1,0:T(8,128)(2,1)}, u32[]{:S(2)}) copy-start(bf16[3,3,3,64,64]{4,3,2,1,0:T(8,128)(2,1)} %param.10) | copy-start | bytes 663556
  0.7 4.7 %copy-start.2 = (bf16[1,2,32,4096]{3,2,1,0:T(8,128)(2,1)S(1)}, bf16[1,2,32,4096]{3,2,1,0:T(8,128)(2,1)}, u32[]{:S(2)}) copy-start(bf16[1,2,32,4096]{3,2,1,0:T(8,128)(2,1)} %param.13) | copy-start | bytes 1572868
  0.7 4.7 %copy-start.3 = (bf16[1,2,32,4096]{3,2,1,0:T(8,128)(2,1)S(1)}, bf16[1,2,32,4096]{3,2,1,0:T(8,128)(2,1)}, u32[]{:S(2)}) copy-start(bf16[1,2,32,4096]{3,2,1,0:T(8,128)(2,1)} %param.7) | copy-start | bytes 1572868
  0.7 4.7 %copy-start.4 = (bf16[1,2,32,4096]{3,2,1,0:T(8,128)(2,1)S(1)}, bf16[1,2,32,4096]{3,2,1,0:T(8,128)(2,1)}, u32[]{:S(2)}) copy-start(bf16[1,2,32,4096]{3,2,1,0:T(8,128)(2,1)} %param.9) | copy-start | bytes 1572868
  2.1 15.0 %collective-permute-start = (bf16[2,32,4096]{2,1,0:T(8,128)(2,1)S(1)}, bf16[2,32,4096]{2,1,0:T(8,128)(2,1)S(1)}, u32[]{:S(2)}, u32[]{:S(2)}) collective-permute-start(bf16[2,32,4096]{2,1,0:T(8,128)(2,1)S(1)} %broadcast_select_fusion), channel_id=1, source_target_pairs={{0,1},{1,0},{2,3},{3,2},{4,5},{5,4},{6,7},{7,6},{8,9},{9,8},{10,11... | collective-permute-start | bytes 1572872 | tf_op jit(solution)/shard_map/ppermute | solution.py:425
  5.4 1.0 %copy-start = (bf16[1,2,32,4096]{3,2,1,0:T(8,128)(2,1)S(1)}, bf16[1,2,32,4096]{3,2,1,0:T(8,128)(2,1)}, u32[]{:S(2)}) copy-start(bf16[1,2,32,4096]{3,2,1,0:T(8,128)(2,1)} %param.8) | copy-start | bytes 1572868
  6.4 10.7 %copy-start.1 = (f32[64]{0:T(128)S(1)}, f32[64]{0:T(128)}, u32[]{:S(2)}) copy-start(f32[64]{0:T(128)} %param.11) | copy-start | bytes 772
  21.1 15.3 %collective-permute-start.1 = (bf16[2,32,4096]{2,1,0:T(8,128)(2,1)}, bf16[2,32,4096]{2,1,0:T(8,128)(2,1)}, u32[]{:S(2)}, u32[]{:S(2)}) collective-permute-start(bf16[2,32,4096]{2,1,0:T(8,128)(2,1)} %get-tuple-element.25.pre_grad_ref), channel_id=1, source_target_pairs={{1,0},{3,2},{5,4},{7,6},{9,8},{11,10},{13,12},{15,14},{17,16},{19,... | collective-permute-start | bytes 1572872 | tf_op jit(solution)/shard_map/ppermute | solution.py:498
  27.4 23.3 %all-to-all-start = ((bf16[32,56,128]{2,1,0:T(8,128)(2,1)}), bf16[32,56,128]{2,1,0:T(8,128)(2,1)}, u32[]{:S(2)}, u32[]{:S(2)}) async-start(bf16[32,56,128]{2,1,0:T(8,128)(2,1)} %bitcast.11), calls=%async_computation | async-start | bytes 917504 | tf_op jit(solution)/shard_map/all_to_all | solution.py:509
  42.4 15.7 %collective-permute-start.2 = (bf16[4,16,4096]{2,1,0:T(8,128)(2,1)S(1)}, bf16[4,16,4096]{2,1,0:T(8,128)(2,1)S(1)}, u32[]{:S(2)}, u32[]{:S(2)}) collective-permute-start(bf16[4,16,4096]{2,1,0:T(8,128)(2,1)S(1)} %slice.28), channel_id=1, source_target_pairs={{0,1},{2,3},{4,5},{6,7},{8,9},{10,11},{12,13},{14,15},{16,17},{18,... | collective-permute-start | bytes 1572872 | tf_op jit(solution)/shard_map/ppermute | solution.py:400
  52.5 12.5 %all-to-all-start.1 = ((bf16[16,56,128]{2,1,0:T(8,128)(2,1)}), bf16[16,56,128]{2,1,0:T(8,128)(2,1)S(1)}, u32[]{:S(2)}, u32[]{:S(2)}) async-start(bf16[16,56,128]{2,1,0:T(8,128)(2,1)} %share.1), calls=%async_computation.1 | async-start | bytes 458752 | tf_op jit(solution)/shard_map/all_to_all | solution.py:521
  65.0 1.5 %collective-permute-start.3 = (bf16[896,128]{1,0:T(8,128)(2,1)S(1)}, bf16[896,128]{1,0:T(8,128)(2,1)S(1)}, u32[]{:S(2)}, u32[]{:S(2)}) collective-permute-start(bf16[896,128]{1,0:T(8,128)(2,1)S(1)} %bitcast.26), channel_id=1, source_target_pairs={{0,2},{2,0},{1,3},{3,1},{4,6},{6,4},{5,7},{7,5},{8,10},{10,8},{9,1... | collective-permute-start | bytes 688136 | tf_op jit(solution)/shard_map/ppermute | solution.py:524
